TPU v7x, 512 devices: a whole 4x8x8 slice. The times are simulated.
512 devices in a mesh: dp: 32 (over x, y), mx: 4 (over z_hi, core), my: 4 (over z_lo).
Axes of the slice: x: 4, y: 8, z: 8 (z_hi: 2, z_lo: 4; z = z_hi * 4 + z_lo), core: 2. Of those that a mesh axis runs over, the one named last changes fastest.
Arguments:
- mentor_final_states: bfloat16 [2048, 4608], P('dp'), may hold values from -12 to 12
- mentor_output_matrix: bfloat16 [4608, 4096], P(None, ('mx', 'my')), may hold values from -0.09375 to 0.09375
- learner_final_states: bfloat16 [2048, 3584], P('dp', 'mx'), may hold values from -12 to 12
- learner_output_matrix: bfloat16 [3584, 4096], P('mx', 'my'), may hold values from -0.09375 to 0.09375
- loss_mask: int32 [2048], P('dp'), may hold values 0 or 1
Outputs:
- mismatch_per_piece: float32 [2048], P('dp')
- mean_loss: float32 [], replicated
- student_grad: float32 [2048, 4096], P('dp', 'my')
All inputs are finite; a program needn't handle non-finite values.
Results may differ from a plain program's by a relative error of at most 0.0003.
Values sent between devices are 32-bit elements.
A program may use at most 64 MiB of HBM per device.

v0:
```python
import functools

import jax
import jax.numpy as jnp
from jax import lax
from jax.experimental import pallas as pl
from jax.experimental.pallas import tpu as pltpu
from jax.sharding import PartitionSpec as P

SOFTENING_HEAT = 2.0
CORES = 2
TEACHER_CHUNKS = 4
MESH = pl.DeviceIdType.MESH


def kernel(
    sizes,
    ts_hbm, tw_hbm, ss_hbm, sw_hbm, mask_ref,
    small_ref, grad_ref,
    ts, tw, ss, sw,
    t_own, t_all, s_all, a_send, own, a_recv, b_send, b_recv,
    st_send, st_all, cnt_all, los_all,
    ld_sem, tt_sem, ag_send, ag_sem, rs_send, rs_sem, bs_send, bs_sem,
    st_ssem, st_rsem, cn_ssem, cn_rsem, lo_ssem, lo_rsem,
):
    n_dp, n_mx, n_my = sizes
    h = n_mx // CORES
    group = n_mx * n_my
    dp, mx, my = lax.axis_index("dp"), lax.axis_index("mx"), lax.axis_index("my")
    yy, cc = mx // CORES, mx % CORES
    me = mx * n_my + my
    partner = {"mx": yy * CORES + (1 - cc)}
    tokens, bc = t_own.shape
    kc = tw.shape[0] // TEACHER_CHUNKS

    def remote(src, dst, ssem, rsem, dev):
        return pltpu.make_async_remote_copy(
            src_ref=src, dst_ref=dst, send_sem=ssem, recv_sem=rsem, device_id=dev, device_id_type=MESH
        )

    loads = [pltpu.make_async_copy(ts_hbm, ts, ld_sem.at[0])]
    for k in range(TEACHER_CHUNKS):
        rows = pl.ds(k * kc, kc)
        loads.append(pltpu.make_async_copy(tw_hbm.at[rows, :], tw.at[rows, :], ld_sem.at[1 + k]))
    base = 1 + TEACHER_CHUNKS
    loads.append(pltpu.make_async_copy(ss_hbm, ss, ld_sem.at[base]))
    for k in range(n_mx):
        r, core = k % h, (1 - cc if k < h else cc)
        block = ((yy + r) % h) * CORES + core
        cols = pl.ds(pl.multiple_of(block * bc, bc), bc)
        loads.append(pltpu.make_async_copy(sw_hbm.at[:, cols], sw.at[k], ld_sem.at[base + 1 + k]))
    for c in loads[:base]:
        c.start()

    barrier = pltpu.get_barrier_semaphore()
    for k in range(1, group):
        peer = (me + k) % group
        pl.semaphore_signal(
            barrier, inc=1, device_id={"mx": peer // n_my, "my": peer % n_my}, device_id_type=MESH
        )
    for k in range(1, n_dp):
        pl.semaphore_signal(barrier, inc=1, device_id={"dp": (dp + k) % n_dp}, device_id_type=MESH)

    mask = mask_ref[...].astype(jnp.float32)
    cnt_all[dp] = jnp.broadcast_to(jnp.sum(mask, axis=1, keepdims=True), cnt_all.shape[1:])

    loads[0].wait()
    acc = jnp.zeros((tokens, bc), jnp.float32)
    for k in range(TEACHER_CHUNKS):
        loads[1 + k].wait()
        if k == 1:
            for c in loads[base:]:
                c.start()
        rows = slice(k * kc, (k + 1) * kc)
        acc += jnp.dot(ts[:, rows], tw[rows, :], preferred_element_type=jnp.float32)
    t_own[...] = acc * (1.0 / SOFTENING_HEAT)

    pl.semaphore_wait(barrier, group - 1 + n_dp - 1)

    swap = remote(t_own, t_all.at[my], tt_sem.at[0], tt_sem.at[1], {"mx": my, "my": mx})

    @pl.when(mx != my)
    def _():
        swap.start()

    @pl.when(mx == my)
    def _():
        t_all[mx] = t_own[...]

    def dp_copies(buf, ssem, rsem):
        return [
            remote(buf.at[dp], buf.at[dp], ssem.at[k], rsem.at[k], {"dp": (dp + k) % n_dp})
            for k in range(1, n_dp)
        ]

    cnt_copies = dp_copies(cnt_all, cn_ssem, cn_rsem)
    for c in cnt_copies:
        c.start()

    loads[base].wait()
    ra = []
    for k in range(n_mx):
        loads[base + 1 + k].wait()
        part = jnp.dot(ss[...], sw[k], preferred_element_type=jnp.float32)
        if k < h:
            a_send[k] = part
            c = remote(a_send.at[k], a_recv.at[k], rs_send.at[k], rs_sem.at[k], partner)
            c.start()
            ra.append(c)
        else:
            own[k - h] = part

    rb = []
    for r in list(range(1, h)) + [0]:
        ra[r].wait_recv()
        if r:
            b_send[r] = own[r] + a_recv[r]
            c = remote(
                b_send.at[r], b_recv.at[r], bs_send.at[r], bs_sem.at[r],
                {"mx": ((yy + r) % h) * CORES + cc},
            )
            c.start()
            rb.append(c)
    total = own[0] + a_recv[0]
    for r, c in enumerate(rb):
        c.wait_recv()
        total = total + b_recv[r + 1]
    s_blk = total * (1.0 / SOFTENING_HEAT)
    s_all[mx] = s_blk

    def gather(buf, which):
        firsts = [remote(buf.at[mx], buf.at[mx], ag_send.at[which, r], ag_sem.at[which, r],
                         {"mx": ((yy + r) % h) * CORES + cc}) for r in range(1, h)]
        pairs = []
        for r in range(h):
            slot = ((yy - r + h) % h) * CORES + cc
            pairs.append(remote(buf.at[slot], buf.at[slot], ag_send.at[which, h + r],
                                ag_sem.at[which, h + r], partner))
        return firsts, pairs

    s_first, s_pair = gather(s_all, 0)
    t_first, t_pair = gather(t_all, 1)
    for c in s_first:
        c.start()
    s_pair[0].start()

    @pl.when(mx != my)
    def _():
        swap.wait_recv()

    for c in t_first:
        c.start()
    t_pair[0].start()

    t_blk = t_all[mx]
    mt = jnp.max(t_blk, axis=1, keepdims=True)
    ms = jnp.max(s_blk, axis=1, keepdims=True)
    td, sd = t_blk - mt, s_blk - ms
    et = jnp.exp(td)
    st = jnp.sum(et, axis=1, keepdims=True)
    sS = jnp.sum(jnp.exp(sd), axis=1, keepdims=True)
    cr = jnp.sum(et * (td - sd), axis=1, keepdims=True)
    lane = lax.broadcasted_iota(jnp.int32, (tokens, 128), 1)
    packed = jnp.where(lane == 0, mt, jnp.where(lane == 1, st, jnp.where(lane == 2, ms, jnp.where(lane == 3, sS, cr))))
    if tokens < 128:
        packed = jnp.concatenate([packed, jnp.zeros((128 - tokens, 128), jnp.float32)], axis=0)
    tile = packed.T[:8, :]
    st_send[...] = tile
    st_all[me] = tile
    st_copies = []
    for k in range(1, group):
        peer = (me + k) % group
        c = remote(st_send, st_all.at[me], st_ssem.at[k], st_rsem.at[k],
                   {"mx": peer // n_my, "my": peer % n_my})
        c.start()
        st_copies.append(c)

    for firsts, pairs in ((s_first, s_pair), (t_first, t_pair)):
        for r, c in enumerate(firsts):
            c.wait_recv()
            pairs[r + 1].start()

    for c in cnt_copies:
        c.wait_recv()
    count = jnp.sum(cnt_all[:, 0:1, :], axis=0)
    for c in st_copies:
        c.wait_recv()
    mts, sts, mss, sss, crs = (st_all[:, i, :] for i in range(5))
    top_t = jnp.max(mts, axis=0, keepdims=True)
    top_s = jnp.max(mss, axis=0, keepdims=True)
    w = jnp.exp(mts - top_t)
    sum_t = jnp.sum(sts * w, axis=0, keepdims=True)
    sum_s = jnp.sum(sss * jnp.exp(mss - top_s), axis=0, keepdims=True)
    d = jnp.sum(w * (crs + sts * ((mts - top_t) - (mss - top_s))), axis=0, keepdims=True)
    log_t, log_s = jnp.log(sum_t), jnp.log(sum_s)
    mism = (SOFTENING_HEAT * SOFTENING_HEAT) * (d / sum_t - log_t + log_s)
    mism = mism[:, :tokens]
    small_ref[0:1, :tokens] = mism
    los_all[dp] = jnp.broadcast_to(jnp.sum(mask * mism, axis=1, keepdims=True), los_all.shape[1:])
    los_copies = dp_copies(los_all, lo_ssem, lo_rsem)
    for c in los_copies:
        c.start()

    multiplier = SOFTENING_HEAT * n_mx * n_my * bc * n_dp * tokens
    mult = mask * multiplier / count[:, :tokens]
    if tokens < 128:
        mult = jnp.concatenate([mult, jnp.zeros((1, 128 - tokens), jnp.float32)], axis=1)
    row = lax.broadcasted_iota(jnp.int32, (128, 128), 0)
    back = jnp.where(row == 0, top_t + log_t, jnp.where(row == 1, top_s + log_s, mult)).T
    lt, ls, mu = back[:tokens, 0:1], back[:tokens, 1:2], back[:tokens, 2:3]

    for c in s_pair + t_pair:
        c.wait_recv()
    for j in range(n_mx):
        grad_ref[:, j * bc:(j + 1) * bc] = (jnp.exp(s_all[j] - ls) - jnp.exp(t_all[j] - lt)) * mu

    for c in los_copies:
        c.wait_recv()
    small_ref[1:2, :] = jnp.sum(los_all[:, 0:1, :], axis=0) / count

    @pl.when(mx != my)
    def _():
        swap.wait_send()

    for c in cnt_copies + los_copies + ra + rb + s_first + s_pair + t_first + t_pair + st_copies:
        c.wait_send()


def deliver(small_ref, grad_ref, mism_ref, loss_ref, out_ref, sem):
    copy = pltpu.make_async_copy(grad_ref, out_ref, sem)
    copy.start()
    mism_ref[...] = small_ref[0:1, :mism_ref.shape[1]]
    loss_ref[...] = small_ref[1:2, 0:1]
    copy.wait()


def shards(sizes, ts, tw, ss, sw, mask):
    n_dp, n_mx, n_my = sizes
    tokens, bc = ts.shape[0], tw.shape[1]
    cols = sw.shape[1]
    h = n_mx // CORES
    group = n_mx * n_my
    f32 = jnp.float32
    V, D = pltpu.VMEM, pltpu.SemaphoreType.DMA
    hbm = pl.BlockSpec(memory_space=pltpu.HBM)
    vm = pl.BlockSpec(memory_space=pltpu.VMEM)
    small, grad = pl.pallas_call(
        functools.partial(kernel, sizes),
        out_shape=(
            V((8, max(tokens, 128)), f32),
            V((tokens, cols), f32),
        ),
        in_specs=[hbm, hbm, hbm, hbm, vm],
        out_specs=(vm, vm),
        scratch_shapes=[
            V(ts.shape, ts.dtype), V(tw.shape, tw.dtype), V(ss.shape, ss.dtype),
            V((n_mx, sw.shape[0], bc), sw.dtype),
            V((tokens, bc), f32), V((n_mx, tokens, bc), f32), V((n_mx, tokens, bc), f32),
            V((h, tokens, bc), f32), V((h, tokens, bc), f32), V((h, tokens, bc), f32),
            V((h, tokens, bc), f32), V((h, tokens, bc), f32),
            V((8, 128), f32), V((group, 8, 128), f32), V((n_dp, 8, 128), f32), V((n_dp, 8, 128), f32),
            D((2 + TEACHER_CHUNKS + n_mx,)), D((2,)),
            D((2, 2 * h)), D((2, 2 * h)), D((h,)), D((h,)), D((h,)), D((h,)),
            D((group,)), D((group,)), D((n_dp,)), D((n_dp,)), D((n_dp,)), D((n_dp,)),
        ],
        compiler_params=pltpu.CompilerParams(
            collective_id=0, has_side_effects=True, vmem_limit_bytes=64_000_000
        ),
    )(ts, tw, ss, sw, mask.reshape(1, tokens))
    mism, loss, grad = pl.pallas_call(
        deliver,
        out_shape=(
            jax.ShapeDtypeStruct((1, tokens), f32),
            jax.ShapeDtypeStruct((1, 1), f32),
            jax.ShapeDtypeStruct((tokens, cols), f32),
        ),
        in_specs=[vm, vm],
        out_specs=(vm, vm, hbm),
        scratch_shapes=[D],
        compiler_params=pltpu.CompilerParams(vmem_limit_bytes=16 * 1024 * 1024),
    )(
        pltpu.with_memory_space_constraint(small, pltpu.VMEM),
        pltpu.with_memory_space_constraint(grad, pltpu.VMEM),
    )
    return mism.reshape(tokens), loss.reshape(()), grad


def solution(mesh):
    sizes = (mesh.shape["dp"], mesh.shape["mx"], mesh.shape["my"])
    placed = (P("dp", None), P(None, ("mx", "my")), P("dp", "mx"), P("mx", "my"), P("dp"))
    return jax.shard_map(
        functools.partial(shards, sizes), mesh=mesh, in_specs=placed,
        out_specs=(P("dp"), P(), P("dp", "my")), check_vma=False,
    )
```

profile of v0, /device:TPU:1, one launch (start us, length us, event | category | flops | bytes accessed | tf_op | source)
XLA Modules:
  0.0 44.7 jit_solution(7569769349111883731)
XLA Ops:
  0.6 42.8 %shard_map.76 = (f32[8,128]{1,0:T(8,128)S(1)}, f32[64,1024]{1,0:T(8,128)S(1)}) custom-call(bf16[64,4608]{1,0:T(8,128)(2,1)} %ts_hbm.1, bf16[4608,256]{1,0:T(8,128)(2,1)} %tw_hbm.1, bf16[64,896]{1,0:T(8,128)(2,1)} %ss_hbm.1, bf16[896,1024]{1,0:T(8,128)(2,1)} %sw_hbm.1, s32[1,64]{1,0:T(1,128)} %bitcast.3), custom_call_target="tpu_custom_call" | custom-call | tf_op jit(solution)/shard_map/pallas_call | solution.py:247
  43.5 1.2 %shard_map.77 = (f32[1,64]{1,0:T(1,128)}, f32[1,1]{1,0:T(1,128)}, f32[64,1024]{1,0:T(8,128)}) custom-call(f32[8,128]{1,0:T(8,128)S(1)} %get-tuple-element.8.small_ref, f32[64,1024]{1,0:T(8,128)S(1)} %get-tuple-element.9.grad_ref), custom_call_target="tpu_custom_call" | custom-call | tf_op jit(solution)/shard_map/pallas_call | solution.py:270
where the time goes:
time: 44.8 us; the launch traced here: 44.7 us
  Pallas kernels  44 us (98%)
  between operations  0.64 us (1%)
    pallas_call x1, Pallas kernels, shards(): pl.pallas_call(functools.partial(kernel, sizes), out_shape=(V((8, max(tok...  42.8 us
    pallas_call x1, Pallas kernels, shards(): pl.pallas_call(deliver, out_shape=(jax.ShapeDtypeStruct((1, tokens), f32)...  1.23 us

commit v1 on v0

v1 whole, which is shorter than its diff:
```python
import functools

import jax
import jax.numpy as jnp
from jax import lax
from jax.experimental import pallas as pl
from jax.experimental.pallas import tpu as pltpu
from jax.sharding import PartitionSpec as P

SOFTENING_HEAT = 2.0
CORES = 2
TEACHER_CHUNKS = 4
MESH = pl.DeviceIdType.MESH


def kernel(
    sizes,
    ts_hbm, tw_hbm, ss_hbm, sw_hbm, mask_hbm,
    small_ref, grad_ref,
    ts, tw, ss, sw, mask_v,
    t_own, t_all, s_all, d_send, d_recv, own, z_send, z_recv,
    st_all, cnt_all, los_all,
    ld_sem, tt_ssem, tt_rsem, dd_ssem, dd_rsem, zz_ssem, zz_rsem,
    ag_ssem, ag_rsem, rl_ssem, rl_rsem, st_ssem, st_rsem, dp_ssem, dp_rsem,
):
    n_dp, n_mx, n_my = sizes
    group = n_mx * n_my
    dp, mx, my = lax.axis_index("dp"), lax.axis_index("mx"), lax.axis_index("my")
    zz, cc = mx // CORES, mx % CORES
    oz, oc = 1 - zz, 1 - cc
    me = mx * n_my + my
    partner = {"mx": zz * CORES + oc}
    across = {"mx": oz * CORES + cc}
    far = oz * CORES + cc
    tokens, bc = t_own.shape
    kc = tw.shape[0] // TEACHER_CHUNKS

    def remote(src, dst, ssem, rsem, dev):
        return pltpu.make_async_remote_copy(
            src_ref=src, dst_ref=dst, send_sem=ssem, recv_sem=rsem, device_id=dev, device_id_type=MESH
        )

    blocks = [oz * CORES + oc, far, zz * CORES + oc, mx]
    student = [pltpu.make_async_copy(ss_hbm, ss, ld_sem.at[0])]
    for k, block in enumerate(blocks):
        cols = pl.ds(pl.multiple_of(block * bc, bc), bc)
        student.append(pltpu.make_async_copy(sw_hbm.at[:, cols], sw.at[k], ld_sem.at[1 + k]))
    base = 1 + n_mx
    teacher = [pltpu.make_async_copy(ts_hbm, ts, ld_sem.at[base])]
    for k in range(TEACHER_CHUNKS):
        rows = pl.ds(k * kc, kc)
        teacher.append(pltpu.make_async_copy(tw_hbm.at[rows, :], tw.at[rows, :], ld_sem.at[base + 1 + k]))
    mask_load = pltpu.make_async_copy(mask_hbm, mask_v, ld_sem.at[base + 1 + TEACHER_CHUNKS])
    for c in student:
        c.start()
    mask_load.start()

    barrier = pltpu.get_barrier_semaphore()
    for k in range(1, group):
        peer = (me + k) % group
        pl.semaphore_signal(
            barrier, inc=1, device_id={"mx": peer // n_my, "my": peer % n_my}, device_id_type=MESH
        )
    for k in range(1, n_dp):
        pl.semaphore_signal(barrier, inc=1, device_id={"dp": (dp + k) % n_dp}, device_id_type=MESH)

    def dot(k):
        student[1 + k].wait()
        return jnp.dot(ss[...], sw[k], preferred_element_type=jnp.float32)

    student[0].wait()
    d_send[0] = dot(0)
    for c in teacher:
        c.start()
    pl.semaphore_wait(barrier, group - 1 + n_dp - 1)
    d_copies = [
        remote(d_send.at[k], d_recv.at[k], dd_ssem.at[k], dd_rsem.at[k], partner) for k in range(2)
    ]
    d_copies[0].start()
    own[0] = dot(1)
    d_send[1] = dot(2)
    d_copies[1].start()
    own[1] = dot(3)
    d_copies[0].wait_recv()
    z_send[...] = own[0] + d_recv[0]
    z_copy = remote(z_send, z_recv, zz_ssem.at[0], zz_rsem.at[0], across)
    z_copy.start()

    def dp_copies(buf, which):
        return [
            remote(buf.at[dp], buf.at[dp], dp_ssem.at[which, k], dp_rsem.at[which, k], {"dp": (dp + k) % n_dp})
            for k in range(1, n_dp)
        ]

    mask_load.wait()
    mask = mask_v[...].astype(jnp.float32)
    cnt_all[dp] = jnp.broadcast_to(jnp.sum(mask, axis=1, keepdims=True), cnt_all.shape[1:])
    cnt_copies = dp_copies(cnt_all, 0)
    for c in cnt_copies:
        c.start()

    teacher[0].wait()
    acc = jnp.zeros((tokens, bc), jnp.float32)
    for k in range(TEACHER_CHUNKS):
        teacher[1 + k].wait()
        rows = slice(k * kc, (k + 1) * kc)
        acc += jnp.dot(ts[:, rows], tw[rows, :], preferred_element_type=jnp.float32)
    t_own[...] = acc * (1.0 / SOFTENING_HEAT)

    mine = mx == my
    swap = remote(t_own, t_all.at[my], tt_ssem.at[0], tt_rsem.at[0], {"mx": my, "my": mx})
    my_far = (1 - my // CORES) * CORES + my % CORES
    swap_far = remote(t_own, t_all.at[my], tt_ssem.at[1], tt_rsem.at[1], {"mx": my_far, "my": mx})

    @pl.when(jnp.logical_not(mine))
    def _():
        swap.start()

    @pl.when(mine)
    def _():
        t_all[mx] = t_own[...]

    d_copies[1].wait_recv()
    near = own[1] + d_recv[1]
    z_copy.wait_recv()
    s_blk = (near + z_recv[...]) * (1.0 / SOFTENING_HEAT)
    s_all[mx] = s_blk

    @pl.when(jnp.logical_not(mine))
    def _():
        swap.wait_recv()

    t_blk = t_all[mx]
    mt = jnp.max(t_blk, axis=1, keepdims=True)
    ms = jnp.max(s_blk, axis=1, keepdims=True)
    td, sd = t_blk - mt, s_blk - ms
    et = jnp.exp(td)
    st = jnp.sum(et, axis=1, keepdims=True)
    sS = jnp.sum(jnp.exp(sd), axis=1, keepdims=True)
    cr = jnp.sum(et * (td - sd), axis=1, keepdims=True)
    log_st, log_ss = jnp.log(st), jnp.log(sS)
    kl = cr / st - log_st + log_ss
    lane = lax.broadcasted_iota(jnp.int32, (tokens, 128), 1)
    upper = jnp.where(lane == 0, mt + log_st, kl)
    lower = jnp.broadcast_to(ms + log_ss, (tokens, 128))
    st_all[me] = jnp.concatenate([upper, lower], axis=0).T[:2, :]
    st_copies = []
    for k in range(1, group):
        peer = (me + k) % group
        c = remote(st_all.at[me], st_all.at[me], st_ssem.at[k], st_rsem.at[k],
                   {"mx": peer // n_my, "my": peer % n_my})
        c.start()
        st_copies.append(c)

    s_far = remote(s_all.at[mx], s_all.at[mx], ag_ssem.at[0], ag_rsem.at[0], across)
    s_far.start()

    swap_far.start()

    relays = [
        remote(buf.at[slot], buf.at[slot], rl_ssem.at[i], rl_rsem.at[i], partner)
        for i, (buf, slot) in enumerate(((s_all, mx), (t_all, mx), (s_all, far), (t_all, far)))
    ]
    relays[0].start()
    relays[1].start()

    for c in cnt_copies:
        c.wait_recv()
    count = jnp.sum(cnt_all[:, 0, :], axis=0, keepdims=True)
    for c in st_copies:
        c.wait_recv()
    both = st_all[:, 0, :]
    kls = st_all[:, 1, :][:, :tokens]
    top = jnp.max(both, axis=0, keepdims=True)
    lse = top + jnp.log(jnp.sum(jnp.exp(both - top), axis=0, keepdims=True))
    rel = both - lse
    rel_t, rel_s = rel[:, :tokens], rel[:, tokens:2 * tokens]
    mism = (SOFTENING_HEAT * SOFTENING_HEAT) * jnp.sum(
        jnp.exp(rel_t) * (kls + (rel_t - rel_s)), axis=0, keepdims=True
    )
    small_ref[0:1, :tokens] = mism
    los_all[dp] = jnp.broadcast_to(jnp.sum(mask * mism, axis=1, keepdims=True), los_all.shape[1:])
    los_copies = dp_copies(los_all, 1)
    for c in los_copies:
        c.start()

    multiplier = SOFTENING_HEAT * n_mx * n_my * bc * n_dp * tokens
    mult = mask * multiplier / count[:, :tokens]
    mult = jnp.concatenate([mult, mult], axis=1)
    row = lax.broadcasted_iota(jnp.int32, (128, 128), 0)
    back = jnp.where(row == 0, lse, mult).T
    lt, ls, mu = back[:tokens, 0:1], back[tokens:2 * tokens, 0:1], back[:tokens, 1:2]

    s_far.wait_recv()
    relays[2].start()

    swap_far.wait_recv()
    relays[3].start()
    for c in relays:
        c.wait_recv()
    for j in range(n_mx):
        grad_ref[:, j * bc:(j + 1) * bc] = (jnp.exp(s_all[j] - ls) - jnp.exp(t_all[j] - lt)) * mu

    for c in los_copies:
        c.wait_recv()
    small_ref[1:2, :] = jnp.sum(los_all[:, 0, :], axis=0, keepdims=True) / count

    @pl.when(jnp.logical_not(mine))
    def _():
        swap.wait_send()

    for c in cnt_copies + los_copies + d_copies + [z_copy, s_far, swap_far] + relays + st_copies:
        c.wait_send()


def deliver(small_ref, grad_ref, mism_ref, loss_ref, out_ref, sem):
    copy = pltpu.make_async_copy(grad_ref, out_ref, sem)
    copy.start()
    mism_ref[...] = small_ref[0:1, :mism_ref.shape[1]]
    loss_ref[...] = small_ref[1:2, 0:1]
    copy.wait()


def shards(sizes, ts, tw, ss, sw, mask):
    n_dp, n_mx, n_my = sizes
    tokens, bc = ts.shape[0], tw.shape[1]
    cols = sw.shape[1]
    group = n_mx * n_my
    f32 = jnp.float32
    V, D = pltpu.VMEM, pltpu.SemaphoreType.DMA
    hbm = pl.BlockSpec(memory_space=pltpu.HBM)
    vm = pl.BlockSpec(memory_space=pltpu.VMEM)
    small, grad = pl.pallas_call(
        functools.partial(kernel, sizes),
        out_shape=(V((8, 128), f32), V((tokens, cols), f32)),
        in_specs=[hbm, hbm, hbm, hbm, hbm],
        out_specs=(vm, vm),
        scratch_shapes=[
            V(ts.shape, ts.dtype), V(tw.shape, tw.dtype), V(ss.shape, ss.dtype),
            V((n_mx, sw.shape[0], bc), sw.dtype), V((1, tokens), mask.dtype),
            V((tokens, bc), f32), V((n_mx, tokens, bc), f32), V((n_mx, tokens, bc), f32),
            V((2, tokens, bc), f32), V((2, tokens, bc), f32), V((2, tokens, bc), f32),
            V((tokens, bc), f32), V((tokens, bc), f32),
            V((group, 2, 128), f32), V((n_dp, 1, 128), f32), V((n_dp, 1, 128), f32),
            D((3 + TEACHER_CHUNKS + n_mx,)), D((2,)), D((2,)), D((2,)), D((2,)), D((1,)), D((1,)),
            D((1,)), D((1,)), D((4,)), D((4,)), D((group,)), D((group,)), D((2, n_dp)), D((2, n_dp)),
        ],
        compiler_params=pltpu.CompilerParams(
            collective_id=0, has_side_effects=True, vmem_limit_bytes=64_000_000
        ),
    )(ts, tw, ss, sw, mask.reshape(1, tokens))
    mism, loss, grad = pl.pallas_call(
        deliver,
        out_shape=(
            jax.ShapeDtypeStruct((1, tokens), f32),
            jax.ShapeDtypeStruct((1, 1), f32),
            jax.ShapeDtypeStruct((tokens, cols), f32),
        ),
        in_specs=[vm, vm],
        out_specs=(vm, vm, hbm),
        scratch_shapes=[D],
        compiler_params=pltpu.CompilerParams(vmem_limit_bytes=16 * 1024 * 1024),
    )(
        pltpu.with_memory_space_constraint(small, pltpu.VMEM),
        pltpu.with_memory_space_constraint(grad, pltpu.VMEM),
    )
    return mism.reshape(tokens), loss.reshape(()), grad


def solution(mesh):
    sizes = (mesh.shape["dp"], mesh.shape["mx"], mesh.shape["my"])
    placed = (P("dp", None), P(None, ("mx", "my")), P("dp", "mx"), P("mx", "my"), P("dp"))
    return jax.shard_map(
        functools.partial(shards, sizes), mesh=mesh, in_specs=placed,
        out_specs=(P("dp"), P(), P("dp", "my")), check_vma=False,
    )
```

time: 44.8 us -> 41.7 us (0.931)
  Pallas kernels: 44 us -> 40.9 us
    pallas_call x1, Pallas kernels: 42.8 us -> 39.6 us  [shards(): pl.pallas_call(functools.partial(kernel, sizes), out_shape=(V((8, 128), f...]
where the time goes in v1:
time: 41.7 us; the launch traced here: 41.5 us
  Pallas kernels  40.9 us (98%)
  between operations  0.64 us (2%)
    pallas_call x1, Pallas kernels, shards(): pl.pallas_call(functools.partial(kernel, sizes), out_shape=(V((8, 128), f...  39.6 us
    pallas_call x1, Pallas kernels, shards(): pl.pallas_call(deliver, out_shape=(jax.ShapeDtypeStruct((1, tokens), f32)...  1.23 us

profile of v1, /device:TPU:1, one launch (start us, length us, event | category | flops | bytes accessed | tf_op | source)
XLA Modules:
  0.0 41.5 jit_solution(14140366944308932803)
XLA Ops:
  0.6 39.6 %shard_map.76 = (f32[8,128]{1,0:T(8,128)S(1)}, f32[64,1024]{1,0:T(8,128)S(1)}) custom-call(bf16[64,4608]{1,0:T(8,128)(2,1)} %ts_hbm.1, bf16[4608,256]{1,0:T(8,128)(2,1)} %tw_hbm.1, bf16[64,896]{1,0:T(8,128)(2,1)} %ss_hbm.1, bf16[896,1024]{1,0:T(8,128)(2,1)} %sw_hbm.1, s32[1,64]{1,0:T(1,128)} %bitcast.3), custom_call_target="tpu_custom_call" | custom-call | tf_op jit(solution)/shard_map/pallas_call | solution.py:233
  40.3 1.2 %shard_map.77 = (f32[1,64]{1,0:T(1,128)}, f32[1,1]{1,0:T(1,128)}, f32[64,1024]{1,0:T(8,128)}) custom-call(f32[8,128]{1,0:T(8,128)S(1)} %get-tuple-element.8.small_ref, f32[64,1024]{1,0:T(8,128)S(1)} %get-tuple-element.9.grad_ref), custom_call_target="tpu_custom_call" | custom-call | tf_op jit(solution)/shard_map/pallas_call | solution.py:252

commit v2 on v1

--- a/solution.py
+++ b/solution.py
@@ -18,10 +18,9 @@
     ts_hbm, tw_hbm, ss_hbm, sw_hbm, mask_hbm,
     small_ref, grad_ref,
     ts, tw, ss, sw, mask_v,
-    t_own, t_all, s_all, d_send, d_recv, own, z_send, z_recv,
+    t_own, t_in, d_send, d_recv, own, z_send, z_recv,
     st_all, cnt_all, los_all,
-    ld_sem, tt_ssem, tt_rsem, dd_ssem, dd_rsem, zz_ssem, zz_rsem,
-    ag_ssem, ag_rsem, rl_ssem, rl_rsem, st_ssem, st_rsem, dp_ssem, dp_rsem,
+    ld_sem, tt_sem, dd_ssem, dd_rsem, zz_sem, ag_sem, rl_ssem, rl_rsem, st_sem, dp_ssem, dp_rsem,
 ):
     n_dp, n_mx, n_my = sizes
     group = n_mx * n_my
@@ -83,21 +82,19 @@
     own[1] = dot(3)
     d_copies[0].wait_recv()
     z_send[...] = own[0] + d_recv[0]
-    z_copy = remote(z_send, z_recv, zz_ssem.at[0], zz_rsem.at[0], across)
+    z_copy = remote(z_send, z_recv, zz_sem.at[0], zz_sem.at[1], across)
     z_copy.start()
 
-    def dp_copies(buf, which):
-        return [
-            remote(buf.at[dp], buf.at[dp], dp_ssem.at[which, k], dp_rsem.at[which, k], {"dp": (dp + k) % n_dp})
-            for k in range(1, n_dp)
-        ]
+    def dp_send(buf, which):
+        for k in range(1, n_dp):
+            remote(buf.at[dp], buf.at[dp], dp_ssem.at[which], dp_rsem.at[which], {"dp": (dp + k) % n_dp}).start()
+        others = buf.at[pl.ds(0, n_dp - 1)]
+        return remote(others, others, dp_ssem.at[which], dp_rsem.at[which], {"dp": (dp + 1) % n_dp})
 
     mask_load.wait()
     mask = mask_v[...].astype(jnp.float32)
     cnt_all[dp] = jnp.broadcast_to(jnp.sum(mask, axis=1, keepdims=True), cnt_all.shape[1:])
-    cnt_copies = dp_copies(cnt_all, 0)
-    for c in cnt_copies:
-        c.start()
+    counts = dp_send(cnt_all, 0)
 
     teacher[0].wait()
     acc = jnp.zeros((tokens, bc), jnp.float32)
@@ -108,9 +105,7 @@
     t_own[...] = acc * (1.0 / SOFTENING_HEAT)
 
     mine = mx == my
-    swap = remote(t_own, t_all.at[my], tt_ssem.at[0], tt_rsem.at[0], {"mx": my, "my": mx})
-    my_far = (1 - my // CORES) * CORES + my % CORES
-    swap_far = remote(t_own, t_all.at[my], tt_ssem.at[1], tt_rsem.at[1], {"mx": my_far, "my": mx})
+    swap = remote(t_own, t_in, tt_sem.at[0], tt_sem.at[1], {"mx": my, "my": mx})
 
     @pl.when(jnp.logical_not(mine))
     def _():
@@ -118,19 +113,18 @@
 
     @pl.when(mine)
     def _():
-        t_all[mx] = t_own[...]
+        t_in[...] = t_own[...]
 
     d_copies[1].wait_recv()
     near = own[1] + d_recv[1]
     z_copy.wait_recv()
     s_blk = (near + z_recv[...]) * (1.0 / SOFTENING_HEAT)
-    s_all[mx] = s_blk
 
     @pl.when(jnp.logical_not(mine))
     def _():
         swap.wait_recv()
 
-    t_blk = t_all[mx]
+    t_blk = t_in[...]
     mt = jnp.max(t_blk, axis=1, keepdims=True)
     ms = jnp.max(s_blk, axis=1, keepdims=True)
     td, sd = t_blk - mt, s_blk - ms
@@ -144,31 +138,16 @@
     upper = jnp.where(lane == 0, mt + log_st, kl)
     lower = jnp.broadcast_to(ms + log_ss, (tokens, 128))
     st_all[me] = jnp.concatenate([upper, lower], axis=0).T[:2, :]
-    st_copies = []
     for k in range(1, group):
         peer = (me + k) % group
-        c = remote(st_all.at[me], st_all.at[me], st_ssem.at[k], st_rsem.at[k],
-                   {"mx": peer // n_my, "my": peer % n_my})
-        c.start()
-        st_copies.append(c)
-
-    s_far = remote(s_all.at[mx], s_all.at[mx], ag_ssem.at[0], ag_rsem.at[0], across)
-    s_far.start()
-
-    swap_far.start()
-
-    relays = [
-        remote(buf.at[slot], buf.at[slot], rl_ssem.at[i], rl_rsem.at[i], partner)
-        for i, (buf, slot) in enumerate(((s_all, mx), (t_all, mx), (s_all, far), (t_all, far)))
-    ]
-    relays[0].start()
-    relays[1].start()
-
-    for c in cnt_copies:
-        c.wait_recv()
+        remote(st_all.at[me], st_all.at[me], st_sem.at[0], st_sem.at[1],
+               {"mx": peer // n_my, "my": peer % n_my}).start()
+    others = st_all.at[pl.ds(0, group - 1)]
+    stats = remote(others, others, st_sem.at[0], st_sem.at[1], partner)
+
+    counts.wait_recv()
     count = jnp.sum(cnt_all[:, 0, :], axis=0, keepdims=True)
-    for c in st_copies:
-        c.wait_recv()
+    stats.wait_recv()
     both = st_all[:, 0, :]
     kls = st_all[:, 1, :][:, :tokens]
     top = jnp.max(both, axis=0, keepdims=True)
@@ -178,11 +157,9 @@
     mism = (SOFTENING_HEAT * SOFTENING_HEAT) * jnp.sum(
         jnp.exp(rel_t) * (kls + (rel_t - rel_s)), axis=0, keepdims=True
     )
+    los_all[dp] = jnp.broadcast_to(jnp.sum(mask * mism, axis=1, keepdims=True), los_all.shape[1:])
+    losses = dp_send(los_all, 1)
     small_ref[0:1, :tokens] = mism
-    los_all[dp] = jnp.broadcast_to(jnp.sum(mask * mism, axis=1, keepdims=True), los_all.shape[1:])
-    los_copies = dp_copies(los_all, 1)
-    for c in los_copies:
-        c.start()
 
     multiplier = SOFTENING_HEAT * n_mx * n_my * bc * n_dp * tokens
     mult = mask * multiplier / count[:, :tokens]
@@ -190,35 +167,46 @@
     row = lax.broadcasted_iota(jnp.int32, (128, 128), 0)
     back = jnp.where(row == 0, lse, mult).T
     lt, ls, mu = back[:tokens, 0:1], back[tokens:2 * tokens, 0:1], back[:tokens, 1:2]
-
-    s_far.wait_recv()
-    relays[2].start()
-
-    swap_far.wait_recv()
-    relays[3].start()
+    grad_ref[mx] = (jnp.exp(s_blk - ls) - jnp.exp(t_blk - lt)) * mu
+
+    g_far = remote(grad_ref.at[mx], grad_ref.at[mx], ag_sem.at[0], ag_sem.at[1], across)
+    relays = [
+        remote(grad_ref.at[slot], grad_ref.at[slot], rl_ssem.at[i], rl_rsem.at[i], partner)
+        for i, slot in enumerate((mx, far))
+    ]
+    g_far.start()
+    relays[0].start()
+    g_far.wait_recv()
+    relays[1].start()
+
+    losses.wait_recv()
+    small_ref[1:2, :] = jnp.sum(los_all[:, 0, :], axis=0, keepdims=True) / count
     for c in relays:
         c.wait_recv()
-    for j in range(n_mx):
-        grad_ref[:, j * bc:(j + 1) * bc] = (jnp.exp(s_all[j] - ls) - jnp.exp(t_all[j] - lt)) * mu
-
-    for c in los_copies:
-        c.wait_recv()
-    small_ref[1:2, :] = jnp.sum(los_all[:, 0, :], axis=0, keepdims=True) / count
 
     @pl.when(jnp.logical_not(mine))
     def _():
         swap.wait_send()
 
-    for c in cnt_copies + los_copies + d_copies + [z_copy, s_far, swap_far] + relays + st_copies:
+    for c in [counts, losses, stats, z_copy, g_far] + d_copies + relays:
         c.wait_send()
 
 
-def deliver(small_ref, grad_ref, mism_ref, loss_ref, out_ref, sem):
-    copy = pltpu.make_async_copy(grad_ref, out_ref, sem)
-    copy.start()
-    mism_ref[...] = small_ref[0:1, :mism_ref.shape[1]]
-    loss_ref[...] = small_ref[1:2, 0:1]
-    copy.wait()
+def deliver(small_ref, grad_ref, mism_out, loss_out, grad_out, mism_v, loss_v, sem):
+    bc = grad_ref.shape[2]
+    copies = [
+        pltpu.make_async_copy(grad_ref.at[j], grad_out.at[:, j * bc:(j + 1) * bc], sem.at[j])
+        for j in range(grad_ref.shape[0])
+    ]
+    for c in copies:
+        c.start()
+    mism_v[...] = small_ref[0:1, :mism_v.shape[1]]
+    loss_v[...] = small_ref[1:2, 0:1]
+    for src, dst in ((mism_v, mism_out), (loss_v, loss_out)):
+        copies.append(pltpu.make_async_copy(src, dst, sem.at[len(copies)]))
+        copies[-1].start()
+    for c in copies:
+        c.wait()
 
 
 def shards(sizes, ts, tw, ss, sw, mask):
@@ -230,20 +218,20 @@
     V, D = pltpu.VMEM, pltpu.SemaphoreType.DMA
     hbm = pl.BlockSpec(memory_space=pltpu.HBM)
     vm = pl.BlockSpec(memory_space=pltpu.VMEM)
-    small, grad = pl.pallas_call(
+    held = pl.pallas_call(
         functools.partial(kernel, sizes),
-        out_shape=(V((8, 128), f32), V((tokens, cols), f32)),
+        out_shape=(V((8, 128), f32), V((n_mx, tokens, bc), f32)),
         in_specs=[hbm, hbm, hbm, hbm, hbm],
         out_specs=(vm, vm),
         scratch_shapes=[
             V(ts.shape, ts.dtype), V(tw.shape, tw.dtype), V(ss.shape, ss.dtype),
             V((n_mx, sw.shape[0], bc), sw.dtype), V((1, tokens), mask.dtype),
-            V((tokens, bc), f32), V((n_mx, tokens, bc), f32), V((n_mx, tokens, bc), f32),
+            V((tokens, bc), f32), V((tokens, bc), f32),
             V((2, tokens, bc), f32), V((2, tokens, bc), f32), V((2, tokens, bc), f32),
             V((tokens, bc), f32), V((tokens, bc), f32),
             V((group, 2, 128), f32), V((n_dp, 1, 128), f32), V((n_dp, 1, 128), f32),
-            D((3 + TEACHER_CHUNKS + n_mx,)), D((2,)), D((2,)), D((2,)), D((2,)), D((1,)), D((1,)),
-            D((1,)), D((1,)), D((4,)), D((4,)), D((group,)), D((group,)), D((2, n_dp)), D((2, n_dp)),
+            D((3 + TEACHER_CHUNKS + n_mx,)), D((2,)), D((2,)), D((2,)), D((2,)), D((2,)),
+            D((2,)), D((2,)), D((2,)), D((2,)), D((2,)),
         ],
         compiler_params=pltpu.CompilerParams(
             collective_id=0, has_side_effects=True, vmem_limit_bytes=64_000_000
@@ -257,13 +245,10 @@
             jax.ShapeDtypeStruct((tokens, cols), f32),
         ),
         in_specs=[vm, vm],
-        out_specs=(vm, vm, hbm),
-        scratch_shapes=[D],
+        out_specs=(hbm, hbm, hbm),
+        scratch_shapes=[V((1, tokens), f32), V((1, 1), f32), D((2 + n_mx,))],
         compiler_params=pltpu.CompilerParams(vmem_limit_bytes=16 * 1024 * 1024),
-    )(
-        pltpu.with_memory_space_constraint(small, pltpu.VMEM),
-        pltpu.with_memory_space_constraint(grad, pltpu.VMEM),
-    )
+    )(*[pltpu.with_memory_space_constraint(x, pltpu.VMEM) for x in held])
     return mism.reshape(tokens), loss.reshape(()), grad
 
 

time: 41.7 us -> 40.5 us (0.971)
  Pallas kernels: 40.9 us -> 39.7 us
    pallas_call x1, Pallas kernels: 39.6 us -> 38.9 us  [shards(): pl.pallas_call(functools.partial(kernel, sizes), out_shape=(V((8, 128), f...]
    pallas_call x1, Pallas kernels: 1.23 us -> 0.75 us  [shards(): pl.pallas_call(deliver, out_shape=(jax.ShapeDtypeStruct((1, tokens), f32)...]
where the time goes in v2:
time: 40.5 us; the launch traced here: 40.3 us
  Pallas kernels  39.7 us (98%)
  between operations  0.64 us (2%)
    pallas_call x1, Pallas kernels, shards(): pl.pallas_call(functools.partial(kernel, sizes), out_shape=(V((8, 128), f...  38.9 us

profile of v2, /device:TPU:1, one launch (start us, length us, event | category | flops | bytes accessed | tf_op | source)
XLA Modules:
  0.0 40.3 jit_solution(2252757370523483414)
XLA Ops:
  0.6 38.9 %shard_map.76 = (f32[8,128]{1,0:T(8,128)S(1)}, f32[4,64,256]{2,1,0:T(8,128)S(1)}) custom-call(bf16[64,4608]{1,0:T(8,128)(2,1)} %ts_hbm.1, bf16[4608,256]{1,0:T(8,128)(2,1)} %tw_hbm.1, bf16[64,896]{1,0:T(8,128)(2,1)} %ss_hbm.1, bf16[896,1024]{1,0:T(8,128)(2,1)} %sw_hbm.1, s32[1,64]{1,0:T(1,128)} %bitcast.3), custom_call_target="tpu_custom_call" | custom-call | tf_op jit(solution)/shard_map/pallas_call | solution.py:221
  39.6 0.8 %shard_map.77 = (f32[1,64]{1,0:T(1,128)}, f32[1,1]{1,0:T(1,128)}, f32[64,1024]{1,0:T(8,128)}) custom-call(f32[8,128]{1,0:T(8,128)S(1)} %get-tuple-element.8.small_ref, f32[4,64,256]{2,1,0:T(8,128)S(1)} %get-tuple-element.9.grad_ref), custom_call_target="tpu_custom_call" | custom-call | tf_op jit(solution)/shard_map/pallas_call | solution.py:240

commit v3 on v2

--- a/solution.py
+++ b/solution.py
@@ -9,6 +9,7 @@
 
 SOFTENING_HEAT = 2.0
 CORES = 2
+RING_Y = 8
 TEACHER_CHUNKS = 4
 MESH = pl.DeviceIdType.MESH
 
@@ -20,12 +21,12 @@
     ts, tw, ss, sw, mask_v,
     t_own, t_in, d_send, d_recv, own, z_send, z_recv,
     st_all, cnt_all, los_all,
-    ld_sem, tt_sem, dd_ssem, dd_rsem, zz_sem, ag_sem, rl_ssem, rl_rsem, st_sem, dp_ssem, dp_rsem,
+    ld_sem, tt_sem, dd_ssem, dd_rsem, zz_sem, ag_sem, rl_ssem, rl_rsem, st_sem, dp_ssem, dp_rsem, token,
 ):
     n_dp, n_mx, n_my = sizes
     group = n_mx * n_my
     dp, mx, my = lax.axis_index("dp"), lax.axis_index("mx"), lax.axis_index("my")
-    zz, cc = mx // CORES, mx % CORES
+    zz, cc = lax.div(mx, CORES), lax.rem(mx, CORES)
     oz, oc = 1 - zz, 1 - cc
     me = mx * n_my + my
     partner = {"mx": zz * CORES + oc}
@@ -54,71 +55,114 @@
         c.start()
     mask_load.start()
 
+    line = [
+        {"mx": lax.rem(mx + i, n_mx), "my": lax.rem(my + j, n_my)}
+        for i in (2, 3, 1, 0) for j in range(n_my) if (i, j) != (0, 0)
+    ]
+    ring_x = n_dp // RING_Y
+    px, py = lax.div(dp, RING_Y), lax.rem(dp, RING_Y)
+
+    def plane(i, j):
+        return {"dp": lax.rem(px + i, ring_x) * RING_Y + lax.rem(py + j, RING_Y)}
+
+    near = [plane(1, 0), plane(ring_x - 1, 0), plane(0, 1), plane(0, RING_Y - 1)]
+
+    def tell(sem, devices):
+        for device in devices:
+            pl.semaphore_signal(sem, inc=1, device_id=device, device_id_type=MESH)
+
     barrier = pltpu.get_barrier_semaphore()
-    for k in range(1, group):
-        peer = (me + k) % group
-        pl.semaphore_signal(
-            barrier, inc=1, device_id={"mx": peer // n_my, "my": peer % n_my}, device_id_type=MESH
-        )
-    for k in range(1, n_dp):
-        pl.semaphore_signal(barrier, inc=1, device_id={"dp": (dp + k) % n_dp}, device_id_type=MESH)
+    tell(barrier, line + near)
 
     def dot(k):
         student[1 + k].wait()
         return jnp.dot(ss[...], sw[k], preferred_element_type=jnp.float32)
 
+    d_copies = [
+        remote(d_send.at[k], d_recv.at[k], dd_ssem.at[k], dd_rsem.at[k], partner) for k in range(2)
+    ]
+    mine = mx == my
+    swap = remote(t_own, t_in, tt_sem.at[0], tt_sem.at[1], {"mx": my, "my": mx})
+
+    def teacher_block():
+        teacher[0].wait()
+        acc = jnp.zeros((tokens, bc), jnp.float32)
+        for k in range(TEACHER_CHUNKS):
+            teacher[1 + k].wait()
+            rows = slice(k * kc, (k + 1) * kc)
+            acc += jnp.dot(ts[:, rows], tw[rows, :], preferred_element_type=jnp.float32)
+        t_own[...] = acc * (1.0 / SOFTENING_HEAT)
+
+    def hand_over():
+        @pl.when(jnp.logical_not(mine))
+        def _():
+            swap.start()
+
+        @pl.when(mine)
+        def _():
+            t_in[...] = t_own[...]
+
+    first, last = zz == 0, zz != 0
     student[0].wait()
     d_send[0] = dot(0)
     for c in teacher:
         c.start()
-    pl.semaphore_wait(barrier, group - 1 + n_dp - 1)
-    d_copies = [
-        remote(d_send.at[k], d_recv.at[k], dd_ssem.at[k], dd_rsem.at[k], partner) for k in range(2)
-    ]
+
+    @pl.when(first)
+    def _():
+        own[0] = dot(1)
+        d_send[1] = dot(2)
+        own[1] = dot(3)
+        teacher_block()
+
+    pl.semaphore_wait(barrier, len(line) + len(near))
     d_copies[0].start()
-    own[0] = dot(1)
-    d_send[1] = dot(2)
-    d_copies[1].start()
-    own[1] = dot(3)
+    tell(token.at[0], near)
+
+    @pl.when(first)
+    def _():
+        d_copies[1].start()
+        hand_over()
+
+    @pl.when(last)
+    def _():
+        own[0] = dot(1)
+        d_send[1] = dot(2)
+        d_copies[1].start()
+        own[1] = dot(3)
+
     d_copies[0].wait_recv()
     z_send[...] = own[0] + d_recv[0]
     z_copy = remote(z_send, z_recv, zz_sem.at[0], zz_sem.at[1], across)
     z_copy.start()
 
+    @pl.when(last)
+    def _():
+        teacher_block()
+        hand_over()
+
+    pl.semaphore_wait(token.at[0], len(near))
+    tell(token.at[1], [plane(0, 2), plane(0, RING_Y - 2)])
+    pl.semaphore_wait(token.at[1], 2)
+    tell(token.at[2], [plane(i, 0) for i in range(1, ring_x)])
+    pl.semaphore_wait(token.at[2], ring_x - 1)
+
     def dp_send(buf, which):
         for k in range(1, n_dp):
-            remote(buf.at[dp], buf.at[dp], dp_ssem.at[which], dp_rsem.at[which], {"dp": (dp + k) % n_dp}).start()
+            peer = {"dp": lax.rem(dp + k, n_dp)}
+            remote(buf.at[dp], buf.at[dp], dp_ssem.at[which], dp_rsem.at[which], peer).start()
         others = buf.at[pl.ds(0, n_dp - 1)]
-        return remote(others, others, dp_ssem.at[which], dp_rsem.at[which], {"dp": (dp + 1) % n_dp})
+        return remote(others, others, dp_ssem.at[which], dp_rsem.at[which], partner)
 
     mask_load.wait()
     mask = mask_v[...].astype(jnp.float32)
     cnt_all[dp] = jnp.broadcast_to(jnp.sum(mask, axis=1, keepdims=True), cnt_all.shape[1:])
     counts = dp_send(cnt_all, 0)
 
-    teacher[0].wait()
-    acc = jnp.zeros((tokens, bc), jnp.float32)
-    for k in range(TEACHER_CHUNKS):
-        teacher[1 + k].wait()
-        rows = slice(k * kc, (k + 1) * kc)
-        acc += jnp.dot(ts[:, rows], tw[rows, :], preferred_element_type=jnp.float32)
-    t_own[...] = acc * (1.0 / SOFTENING_HEAT)
-
-    mine = mx == my
-    swap = remote(t_own, t_in, tt_sem.at[0], tt_sem.at[1], {"mx": my, "my": mx})
-
-    @pl.when(jnp.logical_not(mine))
-    def _():
-        swap.start()
-
-    @pl.when(mine)
-    def _():
-        t_in[...] = t_own[...]
-
     d_copies[1].wait_recv()
-    near = own[1] + d_recv[1]
+    mine_sum = own[1] + d_recv[1]
     z_copy.wait_recv()
-    s_blk = (near + z_recv[...]) * (1.0 / SOFTENING_HEAT)
+    s_blk = (mine_sum + z_recv[...]) * (1.0 / SOFTENING_HEAT)
 
     @pl.when(jnp.logical_not(mine))
     def _():
@@ -138,15 +182,11 @@
     upper = jnp.where(lane == 0, mt + log_st, kl)
     lower = jnp.broadcast_to(ms + log_ss, (tokens, 128))
     st_all[me] = jnp.concatenate([upper, lower], axis=0).T[:2, :]
-    for k in range(1, group):
-        peer = (me + k) % group
-        remote(st_all.at[me], st_all.at[me], st_sem.at[0], st_sem.at[1],
-               {"mx": peer // n_my, "my": peer % n_my}).start()
+    for device in line:
+        remote(st_all.at[me], st_all.at[me], st_sem.at[0], st_sem.at[1], device).start()
     others = st_all.at[pl.ds(0, group - 1)]
     stats = remote(others, others, st_sem.at[0], st_sem.at[1], partner)
 
-    counts.wait_recv()
-    count = jnp.sum(cnt_all[:, 0, :], axis=0, keepdims=True)
     stats.wait_recv()
     both = st_all[:, 0, :]
     kls = st_all[:, 1, :][:, :tokens]
@@ -161,6 +201,8 @@
     losses = dp_send(los_all, 1)
     small_ref[0:1, :tokens] = mism
 
+    counts.wait_recv()
+    count = jnp.sum(cnt_all[:, 0, :], axis=0, keepdims=True)
     multiplier = SOFTENING_HEAT * n_mx * n_my * bc * n_dp * tokens
     mult = mask * multiplier / count[:, :tokens]
     mult = jnp.concatenate([mult, mult], axis=1)
@@ -231,7 +273,7 @@
             V((tokens, bc), f32), V((tokens, bc), f32),
             V((group, 2, 128), f32), V((n_dp, 1, 128), f32), V((n_dp, 1, 128), f32),
             D((3 + TEACHER_CHUNKS + n_mx,)), D((2,)), D((2,)), D((2,)), D((2,)), D((2,)),
-            D((2,)), D((2,)), D((2,)), D((2,)), D((2,)),
+            D((2,)), D((2,)), D((2,)), D((2,)), D((2,)), pltpu.SemaphoreType.REGULAR((3,)),
         ],
         compiler_params=pltpu.CompilerParams(
             collective_id=0, has_side_effects=True, vmem_limit_bytes=64_000_000

time: 40.5 us -> 37 us (0.914)
  Pallas kernels: 39.7 us -> 36.2 us
    pallas_call x1, Pallas kernels: 38.9 us -> 35.5 us  [shards(): pl.pallas_call(functools.partial(kernel, sizes), out_shape=(V((8, 128), f...]
where the time goes in v3:
time: 37 us; the launch traced here: 36.9 us
  Pallas kernels  36.2 us (98%)
  between operations  0.64 us (2%)
    pallas_call x1, Pallas kernels, shards(): pl.pallas_call(functools.partial(kernel, sizes), out_shape=(V((8, 128), f...  35.5 us
    pallas_call x1, Pallas kernels, shards(): pl.pallas_call(deliver, out_shape=(jax.ShapeDtypeStruct((1, tokens), f32)...  0.75 us

profile of v3, /device:TPU:1, one launch (start us, length us, event | category | flops | bytes accessed | tf_op | source)
XLA Modules:
  0.0 36.9 jit_solution(10002480337603336578)
XLA Ops:
  0.6 35.5 %shard_map.76 = (f32[8,128]{1,0:T(8,128)S(1)}, f32[4,64,256]{2,1,0:T(8,128)S(1)}) custom-call(bf16[64,4608]{1,0:T(8,128)(2,1)} %ts_hbm.1, bf16[4608,256]{1,0:T(8,128)(2,1)} %tw_hbm.1, bf16[64,896]{1,0:T(8,128)(2,1)} %ss_hbm.1, bf16[896,1024]{1,0:T(8,128)(2,1)} %sw_hbm.1, s32[1,64]{1,0:T(1,128)} %bitcast.3), custom_call_target="tpu_custom_call" | custom-call | tf_op jit(solution)/shard_map/pallas_call | solution.py:263
  36.1 0.8 %shard_map.77 = (f32[1,64]{1,0:T(1,128)}, f32[1,1]{1,0:T(1,128)}, f32[64,1024]{1,0:T(8,128)}) custom-call(f32[8,128]{1,0:T(8,128)S(1)} %get-tuple-element.8.small_ref, f32[4,64,256]{2,1,0:T(8,128)S(1)} %get-tuple-element.9.grad_ref), custom_call_target="tpu_custom_call" | custom-call | tf_op jit(solution)/shard_map/pallas_call | solution.py:282

commit v4 on v3

--- a/solution.py
+++ b/solution.py
@@ -20,8 +20,8 @@
     small_ref, grad_ref,
     ts, tw, ss, sw, mask_v,
     t_own, t_in, d_send, d_recv, own, z_send, z_recv,
-    st_all, cnt_all, los_all,
-    ld_sem, tt_sem, dd_ssem, dd_rsem, zz_sem, ag_sem, rl_ssem, rl_rsem, st_sem, dp_ssem, dp_rsem, token,
+    st_all, los_all,
+    ld_sem, tt_sem, dd_ssem, dd_rsem, zz_sem, ag_sem, rl_ssem, rl_rsem, st_sem, dp_sem, token,
 ):
     n_dp, n_mx, n_my = sizes
     group = n_mx * n_my
@@ -31,7 +31,13 @@
     me = mx * n_my + my
     partner = {"mx": zz * CORES + oc}
     across = {"mx": oz * CORES + cc}
-    far = oz * CORES + cc
+
+    def block_of(owner, a):
+        one, two = lax.rem(a, 2) * (1 - lax.div(a, 2)), (1 - lax.rem(a, 2)) * lax.div(a, 2)
+        core = lax.rem(owner, CORES)
+        return lax.rem(owner + 2 * (one * (1 - core) + two * core), n_mx)
+
+    owned, far = block_of(mx, my), block_of(oz * CORES + cc, my)
     tokens, bc = t_own.shape
     kc = tw.shape[0] // TEACHER_CHUNKS
 
@@ -40,7 +46,7 @@
             src_ref=src, dst_ref=dst, send_sem=ssem, recv_sem=rsem, device_id=dev, device_id_type=MESH
         )
 
-    blocks = [oz * CORES + oc, far, zz * CORES + oc, mx]
+    blocks = [block_of(oz * CORES + oc, my), far, block_of(zz * CORES + oc, my), owned]
     student = [pltpu.make_async_copy(ss_hbm, ss, ld_sem.at[0])]
     for k, block in enumerate(blocks):
         cols = pl.ds(pl.multiple_of(block * bc, bc), bc)
@@ -71,8 +77,16 @@
         for device in devices:
             pl.semaphore_signal(sem, inc=1, device_id=device, device_id_type=MESH)
 
+    heads = [
+        {"mx": (oz if i else zz) * CORES, "my": lax.rem(my + j, n_my)}
+        for i in (1, 0) for j in range(n_my) if (i, j) != (0, 0)
+    ] + [dict(device, mx=zz * CORES) for device in near]
     barrier = pltpu.get_barrier_semaphore()
-    tell(barrier, line + near)
+    tell(barrier, heads)
+
+    @pl.when(cc == 0)
+    def _():
+        tell(barrier, [partner])
 
     def dot(k):
         student[1 + k].wait()
@@ -82,7 +96,7 @@
         remote(d_send.at[k], d_recv.at[k], dd_ssem.at[k], dd_rsem.at[k], partner) for k in range(2)
     ]
     mine = mx == my
-    swap = remote(t_own, t_in, tt_sem.at[0], tt_sem.at[1], {"mx": my, "my": mx})
+    swap = remote(t_own, t_in, tt_sem.at[0], tt_sem.at[1], {"mx": block_of(my, mx), "my": mx})
 
     def teacher_block():
         teacher[0].wait()
@@ -102,62 +116,57 @@
         def _():
             t_in[...] = t_own[...]
 
-    first, last = zz == 0, zz != 0
+    first = jnp.logical_or(zz == 0, my == 0)
+    last = jnp.logical_not(first)
     student[0].wait()
     d_send[0] = dot(0)
     for c in teacher:
         c.start()
 
+    @pl.when(cc == 1)
+    def _():
+        pl.semaphore_wait(barrier, 1)
+        tell(token.at[3], [partner])
+
+    @pl.when(cc == 0)
+    def _():
+        pl.semaphore_wait(token.at[3], 1)
+
+    d_copies[0].start()
+    own[0] = dot(1)
+    d_send[1] = dot(2)
+    d_copies[1].start()
+    own[1] = dot(3)
+
     @pl.when(first)
     def _():
-        own[0] = dot(1)
-        d_send[1] = dot(2)
-        own[1] = dot(3)
         teacher_block()
-
-    pl.semaphore_wait(barrier, len(line) + len(near))
-    d_copies[0].start()
-    tell(token.at[0], near)
-
-    @pl.when(first)
-    def _():
-        d_copies[1].start()
-        hand_over()
-
-    @pl.when(last)
-    def _():
-        own[0] = dot(1)
-        d_send[1] = dot(2)
-        d_copies[1].start()
-        own[1] = dot(3)
 
     d_copies[0].wait_recv()
     z_send[...] = own[0] + d_recv[0]
     z_copy = remote(z_send, z_recv, zz_sem.at[0], zz_sem.at[1], across)
+
+    @pl.when(cc == 0)
+    def _():
+        pl.semaphore_wait(barrier, CORES * len(heads))
+        tell(token.at[4], [partner])
+
+    @pl.when(cc == 1)
+    def _():
+        pl.semaphore_wait(token.at[4], 1)
+
     z_copy.start()
+
+    @pl.when(first)
+    def _():
+        hand_over()
 
     @pl.when(last)
     def _():
         teacher_block()
         hand_over()
 
-    pl.semaphore_wait(token.at[0], len(near))
-    tell(token.at[1], [plane(0, 2), plane(0, RING_Y - 2)])
-    pl.semaphore_wait(token.at[1], 2)
-    tell(token.at[2], [plane(i, 0) for i in range(1, ring_x)])
-    pl.semaphore_wait(token.at[2], ring_x - 1)
-
-    def dp_send(buf, which):
-        for k in range(1, n_dp):
-            peer = {"dp": lax.rem(dp + k, n_dp)}
-            remote(buf.at[dp], buf.at[dp], dp_ssem.at[which], dp_rsem.at[which], peer).start()
-        others = buf.at[pl.ds(0, n_dp - 1)]
-        return remote(others, others, dp_ssem.at[which], dp_rsem.at[which], partner)
-
-    mask_load.wait()
-    mask = mask_v[...].astype(jnp.float32)
-    cnt_all[dp] = jnp.broadcast_to(jnp.sum(mask, axis=1, keepdims=True), cnt_all.shape[1:])
-    counts = dp_send(cnt_all, 0)
+    tell(token.at[0], near)
 
     d_copies[1].wait_recv()
     mine_sum = own[1] + d_recv[1]
@@ -187,6 +196,14 @@
     others = st_all.at[pl.ds(0, group - 1)]
     stats = remote(others, others, st_sem.at[0], st_sem.at[1], partner)
 
+    pl.semaphore_wait(token.at[0], len(near))
+    tell(token.at[1], [plane(0, 2), plane(0, RING_Y - 2)])
+    pl.semaphore_wait(token.at[1], 2)
+    tell(token.at[2], [plane(i, 0) for i in range(1, ring_x)])
+    mask_load.wait()
+    mask = mask_v[...].astype(jnp.float32)
+    pl.semaphore_wait(token.at[2], ring_x - 1)
+
     stats.wait_recv()
     both = st_all[:, 0, :]
     kls = st_all[:, 1, :][:, :tokens]
@@ -197,41 +214,48 @@
     mism = (SOFTENING_HEAT * SOFTENING_HEAT) * jnp.sum(
         jnp.exp(rel_t) * (kls + (rel_t - rel_s)), axis=0, keepdims=True
     )
-    los_all[dp] = jnp.broadcast_to(jnp.sum(mask * mism, axis=1, keepdims=True), los_all.shape[1:])
-    losses = dp_send(los_all, 1)
+    half = lax.broadcasted_iota(jnp.int32, los_all.shape[1:], 1) < 64
+    los_all[dp] = jnp.where(
+        half, jnp.sum(mask * mism, axis=1, keepdims=True), jnp.sum(mask, axis=1, keepdims=True)
+    )
+    for k in range(1, n_dp):
+        peer = {"dp": lax.rem(dp + k, n_dp)}
+        remote(los_all.at[dp], los_all.at[dp], dp_sem.at[0], dp_sem.at[1], peer).start()
+    others = los_all.at[pl.ds(0, n_dp - 1)]
+    losses = remote(others, others, dp_sem.at[0], dp_sem.at[1], partner)
     small_ref[0:1, :tokens] = mism
 
-    counts.wait_recv()
-    count = jnp.sum(cnt_all[:, 0, :], axis=0, keepdims=True)
-    multiplier = SOFTENING_HEAT * n_mx * n_my * bc * n_dp * tokens
-    mult = mask * multiplier / count[:, :tokens]
+    mult = mask * (SOFTENING_HEAT * n_mx * n_my * bc * n_dp * tokens)
     mult = jnp.concatenate([mult, mult], axis=1)
     row = lax.broadcasted_iota(jnp.int32, (128, 128), 0)
     back = jnp.where(row == 0, lse, mult).T
     lt, ls, mu = back[:tokens, 0:1], back[tokens:2 * tokens, 0:1], back[:tokens, 1:2]
-    grad_ref[mx] = (jnp.exp(s_blk - ls) - jnp.exp(t_blk - lt)) * mu
-
-    g_far = remote(grad_ref.at[mx], grad_ref.at[mx], ag_sem.at[0], ag_sem.at[1], across)
+    grad_ref[owned] = (jnp.exp(s_blk - ls) - jnp.exp(t_blk - lt)) * mu
+
+    g_far = remote(grad_ref.at[owned], grad_ref.at[owned], ag_sem.at[0], ag_sem.at[1], across)
     relays = [
         remote(grad_ref.at[slot], grad_ref.at[slot], rl_ssem.at[i], rl_rsem.at[i], partner)
-        for i, slot in enumerate((mx, far))
+        for i, slot in enumerate((owned, far))
     ]
     g_far.start()
     relays[0].start()
     g_far.wait_recv()
     relays[1].start()
 
-    losses.wait_recv()
-    small_ref[1:2, :] = jnp.sum(los_all[:, 0, :], axis=0, keepdims=True) / count
     for c in relays:
         c.wait_recv()
+    losses.wait_recv()
+    totals = jnp.sum(los_all[:, 0, :], axis=0, keepdims=True)
+    count = totals[:, 64:65]
+    small_ref[1:2, :] = totals / count
 
     @pl.when(jnp.logical_not(mine))
     def _():
         swap.wait_send()
 
-    for c in [counts, losses, stats, z_copy, g_far] + d_copies + relays:
+    for c in [losses, stats, z_copy, g_far] + d_copies + relays:
         c.wait_send()
+    grad_ref[...] = grad_ref[...] * (1.0 / count).reshape(1, 1, 1)
 
 
 def deliver(small_ref, grad_ref, mism_out, loss_out, grad_out, mism_v, loss_v, sem):
@@ -271,9 +295,9 @@
             V((tokens, bc), f32), V((tokens, bc), f32),
             V((2, tokens, bc), f32), V((2, tokens, bc), f32), V((2, tokens, bc), f32),
             V((tokens, bc), f32), V((tokens, bc), f32),
-            V((group, 2, 128), f32), V((n_dp, 1, 128), f32), V((n_dp, 1, 128), f32),
+            V((group, 2, 128), f32), V((n_dp, 1, 128), f32),
             D((3 + TEACHER_CHUNKS + n_mx,)), D((2,)), D((2,)), D((2,)), D((2,)), D((2,)),
-            D((2,)), D((2,)), D((2,)), D((2,)), D((2,)), pltpu.SemaphoreType.REGULAR((3,)),
+            D((2,)), D((2,)), D((2,)), D((2,)), pltpu.SemaphoreType.REGULAR((5,)),
         ],
         compiler_params=pltpu.CompilerParams(
             collective_id=0, has_side_effects=True, vmem_limit_bytes=64_000_000

time: 37 us -> 37.8 us (1.022)
  Pallas kernels: 36.2 us -> 37 us
    pallas_call x1, Pallas kernels: 35.5 us -> 36.3 us  [shards(): pl.pallas_call(functools.partial(kernel, sizes), out_shape=(V((8, 128), f...]
where the time goes in v4:
time: 37.8 us; the launch traced here: 37.7 us
  Pallas kernels  37 us (98%)
  between operations  0.64 us (2%)
    pallas_call x1, Pallas kernels, shards(): pl.pallas_call(functools.partial(kernel, sizes), out_shape=(V((8, 128), f...  36.3 us

profile of v4, /device:TPU:1, one launch (start us, length us, event | category | flops | bytes accessed | tf_op | source)
XLA Modules:
  0.0 37.7 jit_solution(16004741827859890600)
XLA Ops:
  0.6 36.3 %shard_map.76 = (f32[8,128]{1,0:T(8,128)S(1)}, f32[4,64,256]{2,1,0:T(8,128)S(1)}) custom-call(bf16[64,4608]{1,0:T(8,128)(2,1)} %ts_hbm.1, bf16[4608,256]{1,0:T(8,128)(2,1)} %tw_hbm.1, bf16[64,896]{1,0:T(8,128)(2,1)} %ss_hbm.1, bf16[896,1024]{1,0:T(8,128)(2,1)} %sw_hbm.1, s32[1,64]{1,0:T(1,128)} %bitcast.3), custom_call_target="tpu_custom_call" | custom-call | tf_op jit(solution)/shard_map/pallas_call | solution.py:287
  36.9 0.8 %shard_map.77 = (f32[1,64]{1,0:T(1,128)}, f32[1,1]{1,0:T(1,128)}, f32[64,1024]{1,0:T(8,128)}) custom-call(f32[8,128]{1,0:T(8,128)S(1)} %get-tuple-element.8.small_ref, f32[4,64,256]{2,1,0:T(8,128)S(1)} %get-tuple-element.9.grad_ref), custom_call_target="tpu_custom_call" | custom-call | tf_op jit(solution)/shard_map/pallas_call | solution.py:306

commit v5 on v4

--- a/solution.py
+++ b/solution.py
@@ -156,6 +156,7 @@
         pl.semaphore_wait(token.at[4], 1)
 
     z_copy.start()
+    tell(token.at[0], near)
 
     @pl.when(first)
     def _():
@@ -166,7 +167,12 @@
         teacher_block()
         hand_over()
 
-    tell(token.at[0], near)
+    pl.semaphore_wait(token.at[0], len(near))
+    tell(token.at[1], [plane(0, 2), plane(0, RING_Y - 2)])
+    pl.semaphore_wait(token.at[1], 2)
+    tell(token.at[2], [plane(i, 0) for i in range(1, ring_x)])
+    mask_load.wait()
+    mask = mask_v[...].astype(jnp.float32)
 
     d_copies[1].wait_recv()
     mine_sum = own[1] + d_recv[1]
@@ -196,14 +202,6 @@
     others = st_all.at[pl.ds(0, group - 1)]
     stats = remote(others, others, st_sem.at[0], st_sem.at[1], partner)
 
-    pl.semaphore_wait(token.at[0], len(near))
-    tell(token.at[1], [plane(0, 2), plane(0, RING_Y - 2)])
-    pl.semaphore_wait(token.at[1], 2)
-    tell(token.at[2], [plane(i, 0) for i in range(1, ring_x)])
-    mask_load.wait()
-    mask = mask_v[...].astype(jnp.float32)
-    pl.semaphore_wait(token.at[2], ring_x - 1)
-
     stats.wait_recv()
     both = st_all[:, 0, :]
     kls = st_all[:, 1, :][:, :tokens]
@@ -218,9 +216,10 @@
     los_all[dp] = jnp.where(
         half, jnp.sum(mask * mism, axis=1, keepdims=True), jnp.sum(mask, axis=1, keepdims=True)
     )
-    for k in range(1, n_dp):
-        peer = {"dp": lax.rem(dp + k, n_dp)}
-        remote(los_all.at[dp], los_all.at[dp], dp_sem.at[0], dp_sem.at[1], peer).start()
+    pl.semaphore_wait(token.at[2], ring_x - 1)
+    away = [(i, j) for i in range(ring_x) for j in range(RING_Y) if (i, j) != (0, 0)]
+    for i, j in sorted(away, key=lambda p: -min(p[0], ring_x - p[0]) - min(p[1], RING_Y - p[1])):
+        remote(los_all.at[dp], los_all.at[dp], dp_sem.at[0], dp_sem.at[1], plane(i, j)).start()
     others = los_all.at[pl.ds(0, n_dp - 1)]
     losses = remote(others, others, dp_sem.at[0], dp_sem.at[1], partner)
     small_ref[0:1, :tokens] = mism

time: 37.8 us -> 35.2 us (0.931)
  Pallas kernels: 37 us -> 34.4 us
    pallas_call x1, Pallas kernels: 36.3 us -> 33.6 us  [shards(): pl.pallas_call(functools.partial(kernel, sizes), out_shape=(V((8, 128), f...]
where the time goes in v5:
time: 35.2 us; the launch traced here: 35 us
  Pallas kernels  34.4 us (98%)
  between operations  0.64 us (2%)
    pallas_call x1, Pallas kernels, shards(): pl.pallas_call(functools.partial(kernel, sizes), out_shape=(V((8, 128), f...  33.6 us
    pallas_call x1, Pallas kernels, shards(): pl.pallas_call(deliver, out_shape=(jax.ShapeDtypeStruct((1, tokens), f32)...  0.75 us

profile of v5, /device:TPU:1, one launch (start us, length us, event | category | flops | bytes accessed | tf_op | source)
XLA Modules:
  0.0 35.0 jit_solution(4896534421646024297)
XLA Ops:
  0.6 33.6 %shard_map.76 = (f32[8,128]{1,0:T(8,128)S(1)}, f32[4,64,256]{2,1,0:T(8,128)S(1)}) custom-call(bf16[64,4608]{1,0:T(8,128)(2,1)} %ts_hbm.1, bf16[4608,256]{1,0:T(8,128)(2,1)} %tw_hbm.1, bf16[64,896]{1,0:T(8,128)(2,1)} %ss_hbm.1, bf16[896,1024]{1,0:T(8,128)(2,1)} %sw_hbm.1, s32[1,64]{1,0:T(1,128)} %bitcast.3), custom_call_target="tpu_custom_call" | custom-call | tf_op jit(solution)/shard_map/pallas_call | solution.py:286
  34.2 0.8 %shard_map.77 = (f32[1,64]{1,0:T(1,128)}, f32[1,1]{1,0:T(1,128)}, f32[64,1024]{1,0:T(8,128)}) custom-call(f32[8,128]{1,0:T(8,128)S(1)} %get-tuple-element.8.small_ref, f32[4,64,256]{2,1,0:T(8,128)S(1)} %get-tuple-element.9.grad_ref), custom_call_target="tpu_custom_call" | custom-call | tf_op jit(solution)/shard_map/pallas_call | solution.py:305

commit v6 on v5

--- a/solution.py
+++ b/solution.py
@@ -10,7 +10,6 @@
 SOFTENING_HEAT = 2.0
 CORES = 2
 RING_Y = 8
-TEACHER_CHUNKS = 4
 MESH = pl.DeviceIdType.MESH
 
 
@@ -19,9 +18,9 @@
     ts_hbm, tw_hbm, ss_hbm, sw_hbm, mask_hbm,
     small_ref, grad_ref,
     ts, tw, ss, sw, mask_v,
-    t_own, t_in, d_send, d_recv, own, z_send, z_recv,
+    d_send, d_recv, own, z_send, z_recv, g_send,
     st_all, los_all,
-    ld_sem, tt_sem, dd_ssem, dd_rsem, zz_sem, ag_sem, rl_ssem, rl_rsem, st_sem, dp_sem, token,
+    ld_sem, dd_ssem, dd_rsem, zz_ssem, zz_rsem, ag_ssem, ag_rsem, rl_sem, st_sem, dp_sem, token,
 ):
     n_dp, n_mx, n_my = sizes
     group = n_mx * n_my
@@ -30,36 +29,13 @@
     oz, oc = 1 - zz, 1 - cc
     me = mx * n_my + my
     partner = {"mx": zz * CORES + oc}
-    across = {"mx": oz * CORES + cc}
-
-    def block_of(owner, a):
-        one, two = lax.rem(a, 2) * (1 - lax.div(a, 2)), (1 - lax.rem(a, 2)) * lax.div(a, 2)
-        core = lax.rem(owner, CORES)
-        return lax.rem(owner + 2 * (one * (1 - core) + two * core), n_mx)
-
-    owned, far = block_of(mx, my), block_of(oz * CORES + cc, my)
-    tokens, bc = t_own.shape
-    kc = tw.shape[0] // TEACHER_CHUNKS
+    far = oz * CORES + cc
+    tokens, bc = own.shape[1:]
 
     def remote(src, dst, ssem, rsem, dev):
         return pltpu.make_async_remote_copy(
             src_ref=src, dst_ref=dst, send_sem=ssem, recv_sem=rsem, device_id=dev, device_id_type=MESH
         )
-
-    blocks = [block_of(oz * CORES + oc, my), far, block_of(zz * CORES + oc, my), owned]
-    student = [pltpu.make_async_copy(ss_hbm, ss, ld_sem.at[0])]
-    for k, block in enumerate(blocks):
-        cols = pl.ds(pl.multiple_of(block * bc, bc), bc)
-        student.append(pltpu.make_async_copy(sw_hbm.at[:, cols], sw.at[k], ld_sem.at[1 + k]))
-    base = 1 + n_mx
-    teacher = [pltpu.make_async_copy(ts_hbm, ts, ld_sem.at[base])]
-    for k in range(TEACHER_CHUNKS):
-        rows = pl.ds(k * kc, kc)
-        teacher.append(pltpu.make_async_copy(tw_hbm.at[rows, :], tw.at[rows, :], ld_sem.at[base + 1 + k]))
-    mask_load = pltpu.make_async_copy(mask_hbm, mask_v, ld_sem.at[base + 1 + TEACHER_CHUNKS])
-    for c in student:
-        c.start()
-    mask_load.start()
 
     line = [
         {"mx": lax.rem(mx + i, n_mx), "my": lax.rem(my + j, n_my)}
@@ -88,40 +64,35 @@
     def _():
         tell(barrier, [partner])
 
+    blocks = [oz * CORES + oc, far, zz * CORES + oc, mx]
+    student = [pltpu.make_async_copy(ss_hbm, ss, ld_sem.at[0])]
+    for k, block in enumerate(blocks):
+        cols = pl.ds(pl.multiple_of(block * bc, bc), bc)
+        student.append(pltpu.make_async_copy(sw_hbm.at[:, cols], sw.at[k], ld_sem.at[1 + k]))
+    teacher = [
+        pltpu.make_async_copy(ts_hbm, ts, ld_sem.at[1 + n_mx]),
+        pltpu.make_async_copy(tw_hbm, tw, ld_sem.at[2 + n_mx]),
+    ]
+    mask_load = pltpu.make_async_copy(mask_hbm, mask_v, ld_sem.at[3 + n_mx])
+    for c in student:
+        c.start()
+
     def dot(k):
         student[1 + k].wait()
         return jnp.dot(ss[...], sw[k], preferred_element_type=jnp.float32)
 
     d_copies = [
-        remote(d_send.at[k], d_recv.at[k], dd_ssem.at[k], dd_rsem.at[k], partner) for k in range(2)
-    ]
-    mine = mx == my
-    swap = remote(t_own, t_in, tt_sem.at[0], tt_sem.at[1], {"mx": block_of(my, mx), "my": mx})
-
-    def teacher_block():
-        teacher[0].wait()
-        acc = jnp.zeros((tokens, bc), jnp.float32)
-        for k in range(TEACHER_CHUNKS):
-            teacher[1 + k].wait()
-            rows = slice(k * kc, (k + 1) * kc)
-            acc += jnp.dot(ts[:, rows], tw[rows, :], preferred_element_type=jnp.float32)
-        t_own[...] = acc * (1.0 / SOFTENING_HEAT)
-
-    def hand_over():
-        @pl.when(jnp.logical_not(mine))
-        def _():
-            swap.start()
-
-        @pl.when(mine)
-        def _():
-            t_in[...] = t_own[...]
-
-    first = jnp.logical_or(zz == 0, my == 0)
-    last = jnp.logical_not(first)
+        remote(d_send.at[k], d_recv.at[k], dd_ssem.at[0], dd_rsem.at[k], partner) for k in range(2)
+    ]
+    here = mx == my
+    s_near = remote(z_send.at[0], z_recv.at[0], zz_ssem.at[0], zz_rsem.at[0], {"mx": my, "my": mx})
+    s_far = remote(z_send.at[1], z_recv.at[1], zz_ssem.at[1], zz_rsem.at[1], {"mx": my, "my": far})
+
     student[0].wait()
     d_send[0] = dot(0)
     for c in teacher:
         c.start()
+    mask_load.start()
 
     @pl.when(cc == 1)
     def _():
@@ -137,14 +108,8 @@
     d_send[1] = dot(2)
     d_copies[1].start()
     own[1] = dot(3)
-
-    @pl.when(first)
-    def _():
-        teacher_block()
-
     d_copies[0].wait_recv()
-    z_send[...] = own[0] + d_recv[0]
-    z_copy = remote(z_send, z_recv, zz_sem.at[0], zz_sem.at[1], across)
+    z_send[1] = own[0] + d_recv[0]
 
     @pl.when(cc == 0)
     def _():
@@ -155,17 +120,29 @@
     def _():
         pl.semaphore_wait(token.at[4], 1)
 
-    z_copy.start()
+    s_far.start()
+    d_copies[1].wait_recv()
+
+    @pl.when(here)
+    def _():
+        z_recv[0] = own[1] + d_recv[1]
+
+    @pl.when(jnp.logical_not(here))
+    def _():
+        z_send[0] = own[1] + d_recv[1]
+        s_near.start()
+
     tell(token.at[0], near)
 
-    @pl.when(first)
-    def _():
-        hand_over()
-
-    @pl.when(last)
-    def _():
-        teacher_block()
-        hand_over()
+    for c in teacher:
+        c.wait()
+    t_blk = jnp.dot(ts[...], tw[...], preferred_element_type=jnp.float32) * (1.0 / SOFTENING_HEAT)
+    mt = jnp.max(t_blk, axis=1, keepdims=True)
+    td = t_blk - mt
+    et = jnp.exp(td)
+    st = jnp.sum(et, axis=1, keepdims=True)
+    log_st = jnp.log(st)
+    tt = jnp.sum(et * td, axis=1, keepdims=True)
 
     pl.semaphore_wait(token.at[0], len(near))
     tell(token.at[1], [plane(0, 2), plane(0, RING_Y - 2)])
@@ -174,25 +151,16 @@
     mask_load.wait()
     mask = mask_v[...].astype(jnp.float32)
 
-    d_copies[1].wait_recv()
-    mine_sum = own[1] + d_recv[1]
-    z_copy.wait_recv()
-    s_blk = (mine_sum + z_recv[...]) * (1.0 / SOFTENING_HEAT)
-
-    @pl.when(jnp.logical_not(mine))
-    def _():
-        swap.wait_recv()
-
-    t_blk = t_in[...]
-    mt = jnp.max(t_blk, axis=1, keepdims=True)
+    @pl.when(jnp.logical_not(here))
+    def _():
+        s_near.wait_recv()
+
+    s_far.wait_recv()
+    s_blk = (z_recv[0] + z_recv[1]) * (1.0 / SOFTENING_HEAT)
     ms = jnp.max(s_blk, axis=1, keepdims=True)
-    td, sd = t_blk - mt, s_blk - ms
-    et = jnp.exp(td)
-    st = jnp.sum(et, axis=1, keepdims=True)
-    sS = jnp.sum(jnp.exp(sd), axis=1, keepdims=True)
-    cr = jnp.sum(et * (td - sd), axis=1, keepdims=True)
-    log_st, log_ss = jnp.log(st), jnp.log(sS)
-    kl = cr / st - log_st + log_ss
+    sd = s_blk - ms
+    log_ss = jnp.log(jnp.sum(jnp.exp(sd), axis=1, keepdims=True))
+    kl = (tt - jnp.sum(et * sd, axis=1, keepdims=True)) / st - log_st + log_ss
     lane = lax.broadcasted_iota(jnp.int32, (tokens, 128), 1)
     upper = jnp.where(lane == 0, mt + log_st, kl)
     lower = jnp.broadcast_to(ms + log_ss, (tokens, 128))
@@ -229,30 +197,48 @@
     row = lax.broadcasted_iota(jnp.int32, (128, 128), 0)
     back = jnp.where(row == 0, lse, mult).T
     lt, ls, mu = back[:tokens, 0:1], back[tokens:2 * tokens, 0:1], back[:tokens, 1:2]
-    grad_ref[owned] = (jnp.exp(s_blk - ls) - jnp.exp(t_blk - lt)) * mu
-
-    g_far = remote(grad_ref.at[owned], grad_ref.at[owned], ag_sem.at[0], ag_sem.at[1], across)
+    g_send[...] = (jnp.exp(s_blk - ls) - jnp.exp(t_blk - lt)) * mu
+
+    my_far = (1 - lax.div(my, CORES)) * CORES + lax.rem(my, CORES)
+    g_near = remote(g_send, grad_ref.at[my], ag_ssem.at[0], ag_rsem.at[0], {"mx": my, "my": mx})
+    g_far = remote(g_send, grad_ref.at[my], ag_ssem.at[1], ag_rsem.at[1], {"mx": my_far, "my": mx})
+
+    @pl.when(jnp.logical_not(here))
+    def _():
+        g_near.start()
+
+    g_far.start()
+
+    @pl.when(here)
+    def _():
+        grad_ref[mx] = g_send[...]
+
     relays = [
-        remote(grad_ref.at[slot], grad_ref.at[slot], rl_ssem.at[i], rl_rsem.at[i], partner)
-        for i, slot in enumerate((owned, far))
-    ]
-    g_far.start()
+        remote(grad_ref.at[slot], grad_ref.at[slot], rl_sem.at[0], rl_sem.at[1], partner) for slot in (mx, far)
+    ]
+
+    @pl.when(jnp.logical_not(here))
+    def _():
+        g_near.wait_recv()
+
     relays[0].start()
     g_far.wait_recv()
     relays[1].start()
-
-    for c in relays:
-        c.wait_recv()
+    pair = grad_ref.at[pl.ds(0, 2)]
+    relayed = remote(pair, pair, rl_sem.at[0], rl_sem.at[1], partner)
+    relayed.wait_recv()
     losses.wait_recv()
     totals = jnp.sum(los_all[:, 0, :], axis=0, keepdims=True)
     count = totals[:, 64:65]
     small_ref[1:2, :] = totals / count
 
-    @pl.when(jnp.logical_not(mine))
-    def _():
-        swap.wait_send()
-
-    for c in [losses, stats, z_copy, g_far] + d_copies + relays:
+    @pl.when(jnp.logical_not(here))
+    def _():
+        s_near.wait_send()
+        g_near.wait_send()
+
+    halves = remote(d_send, d_recv, dd_ssem.at[0], dd_rsem.at[0], partner)
+    for c in [losses, stats, s_far, g_far, halves, relayed]:
         c.wait_send()
     grad_ref[...] = grad_ref[...] * (1.0 / count).reshape(1, 1, 1)
 
@@ -291,12 +277,11 @@
         scratch_shapes=[
             V(ts.shape, ts.dtype), V(tw.shape, tw.dtype), V(ss.shape, ss.dtype),
             V((n_mx, sw.shape[0], bc), sw.dtype), V((1, tokens), mask.dtype),
-            V((tokens, bc), f32), V((tokens, bc), f32),
             V((2, tokens, bc), f32), V((2, tokens, bc), f32), V((2, tokens, bc), f32),
-            V((tokens, bc), f32), V((tokens, bc), f32),
+            V((2, tokens, bc), f32), V((2, tokens, bc), f32), V((tokens, bc), f32),
             V((group, 2, 128), f32), V((n_dp, 1, 128), f32),
-            D((3 + TEACHER_CHUNKS + n_mx,)), D((2,)), D((2,)), D((2,)), D((2,)), D((2,)),
-            D((2,)), D((2,)), D((2,)), D((2,)), pltpu.SemaphoreType.REGULAR((5,)),
+            D((4 + n_mx,)), D((1,)), D((2,)), D((2,)), D((2,)), D((2,)), D((2,)), D((2,)), D((2,)), D((2,)),
+            pltpu.SemaphoreType.REGULAR((5,)),
         ],
         compiler_params=pltpu.CompilerParams(
             collective_id=0, has_side_effects=True, vmem_limit_bytes=64_000_000

time: 35.2 us -> 34.7 us (0.986)
  Pallas kernels: 34.4 us -> 33.9 us
    pallas_call x1, Pallas kernels: 33.6 us -> 33.2 us  [shards(): pl.pallas_call(functools.partial(kernel, sizes), out_shape=(V((8, 128), f...]
where the time goes in v6:
time: 34.7 us; the launch traced here: 34.6 us
  Pallas kernels  33.9 us (98%)
  between operations  0.64 us (2%)
    pallas_call x1, Pallas kernels, shards(): pl.pallas_call(functools.partial(kernel, sizes), out_shape=(V((8, 128), f...  33.2 us
    pallas_call x1, Pallas kernels, shards(): pl.pallas_call(deliver, out_shape=(jax.ShapeDtypeStruct((1, tokens), f32)...  0.75 us

profile of v6, /device:TPU:1, one launch (start us, length us, event | category | flops | bytes accessed | tf_op | source)
XLA Modules:
  0.0 34.6 jit_solution(17333005432495943609)
XLA Ops:
  0.6 33.2 %shard_map.76 = (f32[8,128]{1,0:T(8,128)S(1)}, f32[4,64,256]{2,1,0:T(8,128)S(1)}) custom-call(bf16[64,4608]{1,0:T(8,128)(2,1)} %ts_hbm.1, bf16[4608,256]{1,0:T(8,128)(2,1)} %tw_hbm.1, bf16[64,896]{1,0:T(8,128)(2,1)} %ss_hbm.1, bf16[896,1024]{1,0:T(8,128)(2,1)} %sw_hbm.1, s32[1,64]{1,0:T(1,128)} %bitcast.3), custom_call_target="tpu_custom_call" | custom-call | tf_op jit(solution)/shard_map/pallas_call | solution.py:272
  33.8 0.8 %shard_map.77 = (f32[1,64]{1,0:T(1,128)}, f32[1,1]{1,0:T(1,128)}, f32[64,1024]{1,0:T(8,128)}) custom-call(f32[8,128]{1,0:T(8,128)S(1)} %get-tuple-element.8.small_ref, f32[4,64,256]{2,1,0:T(8,128)S(1)} %get-tuple-element.9.grad_ref), custom_call_target="tpu_custom_call" | custom-call | tf_op jit(solution)/shard_map/pallas_call | solution.py:290

commit v7 on v6

--- a/solution.py
+++ b/solution.py
@@ -53,12 +53,18 @@
         for device in devices:
             pl.semaphore_signal(sem, inc=1, device_id=device, device_id_type=MESH)
 
-    heads = [
-        {"mx": (oz if i else zz) * CORES, "my": lax.rem(my + j, n_my)}
-        for i in (1, 0) for j in range(n_my) if (i, j) != (0, 0)
-    ] + [dict(device, mx=zz * CORES) for device in near]
+    ring_z = n_mx // CORES * n_my
+    z = zz * n_my + my
+
+    def along(k, core):
+        to = lax.rem(z + k, ring_z)
+        return {"mx": lax.div(to, n_my) * CORES + core, "my": lax.rem(to, n_my)}
+
+    steps = [4, 3, 5, 2, 6]
+    heads = [along(k, 0) for k in steps] + [dict(device, mx=zz * CORES) for device in near]
+    beside = [along(k, 1) for k in (1, ring_z - 1)]
     barrier = pltpu.get_barrier_semaphore()
-    tell(barrier, heads)
+    tell(barrier, heads + beside)
 
     @pl.when(cc == 0)
     def _():
@@ -96,8 +102,9 @@
 
     @pl.when(cc == 1)
     def _():
-        pl.semaphore_wait(barrier, 1)
+        pl.semaphore_wait(barrier, 1 + CORES * len(beside))
         tell(token.at[3], [partner])
+        tell(token.at[5], [along(k, core) for k in (1, ring_z - 1) for core in range(CORES)])
 
     @pl.when(cc == 0)
     def _():
@@ -111,6 +118,31 @@
     d_copies[0].wait_recv()
     z_send[1] = own[0] + d_recv[0]
 
+    def finish_near():
+        d_copies[1].wait_recv()
+
+        @pl.when(here)
+        def _():
+            z_recv[0] = own[1] + d_recv[1]
+
+        @pl.when(jnp.logical_not(here))
+        def _():
+            z_send[0] = own[1] + d_recv[1]
+
+    away_by = lax.rem(lax.div(my, CORES) * n_my + mx + ring_z - z, ring_z)
+    short = jnp.logical_or(away_by <= 2, away_by >= ring_z - 2)
+    soon = jnp.logical_and(short, jnp.logical_or(zz == 0, my == 0))
+
+    @pl.when(soon)
+    def _():
+        finish_near()
+
+    pl.semaphore_wait(token.at[5], len(beside))
+
+    @pl.when(jnp.logical_and(soon, jnp.logical_not(here)))
+    def _():
+        s_near.start()
+
     @pl.when(cc == 0)
     def _():
         pl.semaphore_wait(barrier, CORES * len(heads))
@@ -121,15 +153,13 @@
         pl.semaphore_wait(token.at[4], 1)
 
     s_far.start()
-    d_copies[1].wait_recv()
-
-    @pl.when(here)
-    def _():
-        z_recv[0] = own[1] + d_recv[1]
-
-    @pl.when(jnp.logical_not(here))
-    def _():
-        z_send[0] = own[1] + d_recv[1]
+
+    @pl.when(jnp.logical_not(soon))
+    def _():
+        finish_near()
+
+    @pl.when(jnp.logical_and(jnp.logical_not(soon), jnp.logical_not(here)))
+    def _():
         s_near.start()
 
     tell(token.at[0], near)
@@ -281,7 +311,7 @@
             V((2, tokens, bc), f32), V((2, tokens, bc), f32), V((tokens, bc), f32),
             V((group, 2, 128), f32), V((n_dp, 1, 128), f32),
             D((4 + n_mx,)), D((1,)), D((2,)), D((2,)), D((2,)), D((2,)), D((2,)), D((2,)), D((2,)), D((2,)),
-            pltpu.SemaphoreType.REGULAR((5,)),
+            pltpu.SemaphoreType.REGULAR((6,)),
         ],
         compiler_params=pltpu.CompilerParams(
             collective_id=0, has_side_effects=True, vmem_limit_bytes=64_000_000

time: 34.7 us -> 33.4 us (0.963)
  Pallas kernels: 33.9 us -> 32.6 us
    pallas_call x1, Pallas kernels: 33.2 us -> 31.8 us  [shards(): pl.pallas_call(functools.partial(kernel, sizes), out_shape=(V((8, 128), f...]
where the time goes in v7:
time: 33.4 us; the launch traced here: 33.2 us
  Pallas kernels  32.6 us (98%)
  between operations  0.64 us (2%)
    pallas_call x1, Pallas kernels, shards(): pl.pallas_call(functools.partial(kernel, sizes), out_shape=(V((8, 128), f...  31.8 us
    pallas_call x1, Pallas kernels, shards(): pl.pallas_call(deliver, out_shape=(jax.ShapeDtypeStruct((1, tokens), f32)...  0.75 us

profile of v7, /device:TPU:1, one launch (start us, length us, event | category | flops | bytes accessed | tf_op | source)
XLA Modules:
  0.0 33.2 jit_solution(13011932640736637831)
XLA Ops:
  0.6 31.8 %shard_map.76 = (f32[8,128]{1,0:T(8,128)S(1)}, f32[4,64,256]{2,1,0:T(8,128)S(1)}) custom-call(bf16[64,4608]{1,0:T(8,128)(2,1)} %ts_hbm.1, bf16[4608,256]{1,0:T(8,128)(2,1)} %tw_hbm.1, bf16[64,896]{1,0:T(8,128)(2,1)} %ss_hbm.1, bf16[896,1024]{1,0:T(8,128)(2,1)} %sw_hbm.1, s32[1,64]{1,0:T(1,128)} %bitcast.3), custom_call_target="tpu_custom_call" | custom-call | tf_op jit(solution)/shard_map/pallas_call | solution.py:302
  32.5 0.8 %shard_map.77 = (f32[1,64]{1,0:T(1,128)}, f32[1,1]{1,0:T(1,128)}, f32[64,1024]{1,0:T(8,128)}) custom-call(f32[8,128]{1,0:T(8,128)S(1)} %get-tuple-element.8.small_ref, f32[4,64,256]{2,1,0:T(8,128)S(1)} %get-tuple-element.9.grad_ref), custom_call_target="tpu_custom_call" | custom-call | tf_op jit(solution)/shard_map/pallas_call | solution.py:320

commit v8 on v7

--- a/solution.py
+++ b/solution.py
@@ -60,11 +60,11 @@
         to = lax.rem(z + k, ring_z)
         return {"mx": lax.div(to, n_my) * CORES + core, "my": lax.rem(to, n_my)}
 
+    below, above = lax.div(z + ring_z - 1, ring_z), 1 - lax.div(z + 1, ring_z)
     steps = [4, 3, 5, 2, 6]
     heads = [along(k, 0) for k in steps] + [dict(device, mx=zz * CORES) for device in near]
-    beside = [along(k, 1) for k in (1, ring_z - 1)]
     barrier = pltpu.get_barrier_semaphore()
-    tell(barrier, heads + beside)
+    tell(barrier, heads + [along(ring_z - 1, below), along(1, above)])
 
     @pl.when(cc == 0)
     def _():
@@ -102,9 +102,16 @@
 
     @pl.when(cc == 1)
     def _():
-        pl.semaphore_wait(barrier, 1 + CORES * len(beside))
+        pl.semaphore_wait(barrier, 1 + CORES * (below + above))
         tell(token.at[3], [partner])
-        tell(token.at[5], [along(k, core) for k in (1, ring_z - 1) for core in range(CORES)])
+
+        @pl.when(below == 1)
+        def _():
+            tell(token.at[5], [along(ring_z - 1, core) for core in range(CORES)])
+
+        @pl.when(above == 1)
+        def _():
+            tell(token.at[5], [along(1, core) for core in range(CORES)])
 
     @pl.when(cc == 0)
     def _():
@@ -131,13 +138,12 @@
 
     away_by = lax.rem(lax.div(my, CORES) * n_my + mx + ring_z - z, ring_z)
     short = jnp.logical_or(away_by <= 2, away_by >= ring_z - 2)
-    soon = jnp.logical_and(short, jnp.logical_or(zz == 0, my == 0))
+    soon = jnp.logical_and(short, zz == 0)
 
     @pl.when(soon)
     def _():
         finish_near()
-
-    pl.semaphore_wait(token.at[5], len(beside))
+        pl.semaphore_wait(token.at[5], below + above)
 
     @pl.when(jnp.logical_and(soon, jnp.logical_not(here)))
     def _():
@@ -145,7 +151,7 @@
 
     @pl.when(cc == 0)
     def _():
-        pl.semaphore_wait(barrier, CORES * len(heads))
+        pl.semaphore_wait(barrier, CORES * (len(heads) + 2 - below - above))
         tell(token.at[4], [partner])
 
     @pl.when(cc == 1)
@@ -173,6 +179,10 @@
     st = jnp.sum(et, axis=1, keepdims=True)
     log_st = jnp.log(st)
     tt = jnp.sum(et * td, axis=1, keepdims=True)
+
+    @pl.when(jnp.logical_not(soon))
+    def _():
+        pl.semaphore_wait(token.at[5], below + above)
 
     pl.semaphore_wait(token.at[0], len(near))
     tell(token.at[1], [plane(0, 2), plane(0, RING_Y - 2)])

time: 33.4 us -> 34.1 us (1.021)
  Pallas kernels: 32.6 us -> 33.3 us
    pallas_call x1, Pallas kernels: 31.8 us -> 32.5 us  [shards(): pl.pallas_call(functools.partial(kernel, sizes), out_shape=(V((8, 128), f...]
where the time goes in v8:
time: 34.1 us; the launch traced here: 33.9 us
  Pallas kernels  33.3 us (98%)
  between operations  0.64 us (2%)
    pallas_call x1, Pallas kernels, shards(): pl.pallas_call(functools.partial(kernel, sizes), out_shape=(V((8, 128), f...  32.5 us
    pallas_call x1, Pallas kernels, shards(): pl.pallas_call(deliver, out_shape=(jax.ShapeDtypeStruct((1, tokens), f32)...  0.75 us

profile of v8, /device:TPU:1, one launch (start us, length us, event | category | flops | bytes accessed | tf_op | source)
XLA Modules:
  0.0 33.9 jit_solution(9143618065904359974)
XLA Ops:
  0.6 32.5 %shard_map.76 = (f32[8,128]{1,0:T(8,128)S(1)}, f32[4,64,256]{2,1,0:T(8,128)S(1)}) custom-call(bf16[64,4608]{1,0:T(8,128)(2,1)} %ts_hbm.1, bf16[4608,256]{1,0:T(8,128)(2,1)} %tw_hbm.1, bf16[64,896]{1,0:T(8,128)(2,1)} %ss_hbm.1, bf16[896,1024]{1,0:T(8,128)(2,1)} %sw_hbm.1, s32[1,64]{1,0:T(1,128)} %bitcast.3), custom_call_target="tpu_custom_call" | custom-call | tf_op jit(solution)/shard_map/pallas_call | solution.py:312
  33.2 0.8 %shard_map.77 = (f32[1,64]{1,0:T(1,128)}, f32[1,1]{1,0:T(1,128)}, f32[64,1024]{1,0:T(8,128)}) custom-call(f32[8,128]{1,0:T(8,128)S(1)} %get-tuple-element.8.small_ref, f32[4,64,256]{2,1,0:T(8,128)S(1)} %get-tuple-element.9.grad_ref), custom_call_target="tpu_custom_call" | custom-call | tf_op jit(solution)/shard_map/pallas_call | solution.py:330

commit v9 on v8

--- a/solution.py
+++ b/solution.py
@@ -138,13 +138,26 @@
 
     away_by = lax.rem(lax.div(my, CORES) * n_my + mx + ring_z - z, ring_z)
     short = jnp.logical_or(away_by <= 2, away_by >= ring_z - 2)
-    soon = jnp.logical_and(short, zz == 0)
+    soon = jnp.logical_and(short, jnp.logical_or(zz == 0, my == 0))
+    far_soon = jnp.logical_and(zz == 0, my < 2)
 
     @pl.when(soon)
     def _():
         finish_near()
         pl.semaphore_wait(token.at[5], below + above)
 
+    @pl.when(z == 1)
+    def _():
+        tell(token.at[6], [along(ring_z - 1, cc)])
+
+    @pl.when(z == 0)
+    def _():
+        pl.semaphore_wait(token.at[6], 1)
+
+    @pl.when(far_soon)
+    def _():
+        s_far.start()
+
     @pl.when(jnp.logical_and(soon, jnp.logical_not(here)))
     def _():
         s_near.start()
@@ -158,7 +171,9 @@
     def _():
         pl.semaphore_wait(token.at[4], 1)
 
-    s_far.start()
+    @pl.when(jnp.logical_not(far_soon))
+    def _():
+        s_far.start()
 
     @pl.when(jnp.logical_not(soon))
     def _():
@@ -321,7 +336,7 @@
             V((2, tokens, bc), f32), V((2, tokens, bc), f32), V((tokens, bc), f32),
             V((group, 2, 128), f32), V((n_dp, 1, 128), f32),
             D((4 + n_mx,)), D((1,)), D((2,)), D((2,)), D((2,)), D((2,)), D((2,)), D((2,)), D((2,)), D((2,)),
-            pltpu.SemaphoreType.REGULAR((6,)),
+            pltpu.SemaphoreType.REGULAR((7,)),
         ],
         compiler_params=pltpu.CompilerParams(
             collective_id=0, has_side_effects=True, vmem_limit_bytes=64_000_000

time: 34.1 us -> 33.4 us (0.979)
  Pallas kernels: 33.3 us -> 32.6 us
    pallas_call x1, Pallas kernels: 32.5 us -> 31.8 us  [shards(): pl.pallas_call(functools.partial(kernel, sizes), out_shape=(V((8, 128), f...]
where the time goes in v9:
time: 33.4 us; the launch traced here: 33.2 us
  Pallas kernels  32.6 us (98%)
  between operations  0.64 us (2%)
    pallas_call x1, Pallas kernels, shards(): pl.pallas_call(functools.partial(kernel, sizes), out_shape=(V((8, 128), f...  31.8 us
    pallas_call x1, Pallas kernels, shards(): pl.pallas_call(deliver, out_shape=(jax.ShapeDtypeStruct((1, tokens), f32)...  0.75 us

profile of v9, /device:TPU:1, one launch (start us, length us, event | category | flops | bytes accessed | tf_op | source)
XLA Modules:
  0.0 33.2 jit_solution(1991420256787586046)
XLA Ops:
  0.6 31.8 %shard_map.76 = (f32[8,128]{1,0:T(8,128)S(1)}, f32[4,64,256]{2,1,0:T(8,128)S(1)}) custom-call(bf16[64,4608]{1,0:T(8,128)(2,1)} %ts_hbm.1, bf16[4608,256]{1,0:T(8,128)(2,1)} %tw_hbm.1, bf16[64,896]{1,0:T(8,128)(2,1)} %ss_hbm.1, bf16[896,1024]{1,0:T(8,128)(2,1)} %sw_hbm.1, s32[1,64]{1,0:T(1,128)} %bitcast.3), custom_call_target="tpu_custom_call" | custom-call | tf_op jit(solution)/shard_map/pallas_call | solution.py:327
  32.5 0.8 %shard_map.77 = (f32[1,64]{1,0:T(1,128)}, f32[1,1]{1,0:T(1,128)}, f32[64,1024]{1,0:T(8,128)}) custom-call(f32[8,128]{1,0:T(8,128)S(1)} %get-tuple-element.8.small_ref, f32[4,64,256]{2,1,0:T(8,128)S(1)} %get-tuple-element.9.grad_ref), custom_call_target="tpu_custom_call" | custom-call | tf_op jit(solution)/shard_map/pallas_call | solution.py:345

commit v10 on v9

--- a/solution.py
+++ b/solution.py
@@ -20,7 +20,7 @@
     ts, tw, ss, sw, mask_v,
     d_send, d_recv, own, z_send, z_recv, g_send,
     st_all, los_all,
-    ld_sem, dd_ssem, dd_rsem, zz_ssem, zz_rsem, ag_ssem, ag_rsem, rl_sem, st_sem, dp_sem, token,
+    ld_sem, dd_ssem, dd_rsem, zz_rsem, ag_rsem, rl_sem, st_sem, dp_sem, token,
 ):
     n_dp, n_mx, n_my = sizes
     group = n_mx * n_my
@@ -61,12 +61,19 @@
         return {"mx": lax.div(to, n_my) * CORES + core, "my": lax.rem(to, n_my)}
 
     below, above = lax.div(z + ring_z - 1, ring_z), 1 - lax.div(z + 1, ring_z)
-    steps = [4, 3, 5, 2, 6]
-    heads = [along(k, 0) for k in steps] + [dict(device, mx=zz * CORES) for device in near]
+    upper_low = zz * (1 - lax.div(my, 2))
+
+    def head(k):
+        to = lax.rem(z + k, ring_z)
+        return along(k, 1 - (1 - zz) * lax.div(to, n_my) * (1 - lax.div(lax.rem(to, n_my), 2)))
+
+    heads = [head(k) for k in (4, 3, 5, 2, 6)] + [dict(device, mx=zz * CORES + 1) for device in near]
+    beside = below + above
+    extra = upper_low * (n_my - 1 + my)
     barrier = pltpu.get_barrier_semaphore()
-    tell(barrier, heads + [along(ring_z - 1, below), along(1, above)])
-
-    @pl.when(cc == 0)
+    tell(barrier, heads + [along(ring_z - 1, 1 - below), along(1, 1 - above)])
+
+    @pl.when(cc == 1)
     def _():
         tell(barrier, [partner])
 
@@ -91,8 +98,8 @@
         remote(d_send.at[k], d_recv.at[k], dd_ssem.at[0], dd_rsem.at[k], partner) for k in range(2)
     ]
     here = mx == my
-    s_near = remote(z_send.at[0], z_recv.at[0], zz_ssem.at[0], zz_rsem.at[0], {"mx": my, "my": mx})
-    s_far = remote(z_send.at[1], z_recv.at[1], zz_ssem.at[1], zz_rsem.at[1], {"mx": my, "my": far})
+    s_near = remote(z_send.at[0], z_recv.at[0], ld_sem.at[0], zz_rsem.at[0], {"mx": my, "my": mx})
+    s_far = remote(z_send.at[1], z_recv.at[1], ld_sem.at[1], zz_rsem.at[1], {"mx": my, "my": far})
 
     student[0].wait()
     d_send[0] = dot(0)
@@ -100,20 +107,20 @@
         c.start()
     mask_load.start()
 
-    @pl.when(cc == 1)
-    def _():
-        pl.semaphore_wait(barrier, 1 + CORES * (below + above))
+    @pl.when(cc == 0)
+    def _():
+        pl.semaphore_wait(barrier, 1 + CORES * (beside + extra))
         tell(token.at[3], [partner])
 
         @pl.when(below == 1)
         def _():
-            tell(token.at[5], [along(ring_z - 1, core) for core in range(CORES)])
+            tell(token.at[4], [along(ring_z - 1, core) for core in range(CORES)])
 
         @pl.when(above == 1)
         def _():
-            tell(token.at[5], [along(1, core) for core in range(CORES)])
-
-    @pl.when(cc == 0)
+            tell(token.at[4], [along(1, core) for core in range(CORES)])
+
+    @pl.when(cc == 1)
     def _():
         pl.semaphore_wait(token.at[3], 1)
 
@@ -138,23 +145,30 @@
 
     away_by = lax.rem(lax.div(my, CORES) * n_my + mx + ring_z - z, ring_z)
     short = jnp.logical_or(away_by <= 2, away_by >= ring_z - 2)
-    soon = jnp.logical_and(short, jnp.logical_or(zz == 0, my == 0))
-    far_soon = jnp.logical_and(zz == 0, my < 2)
+    early = jnp.logical_and(zz == 0, short)
+    soon = jnp.logical_or(early, upper_low == 1)
+
+    @pl.when(upper_low == 1)
+    def _():
+        s_far.start()
 
     @pl.when(soon)
     def _():
         finish_near()
-        pl.semaphore_wait(token.at[5], below + above)
+
+    @pl.when(early)
+    def _():
+        pl.semaphore_wait(token.at[4], beside)
 
     @pl.when(z == 1)
     def _():
-        tell(token.at[6], [along(ring_z - 1, cc)])
+        tell(token.at[5], [along(ring_z - 1, cc)])
 
     @pl.when(z == 0)
     def _():
-        pl.semaphore_wait(token.at[6], 1)
-
-    @pl.when(far_soon)
+        pl.semaphore_wait(token.at[5], 1)
+
+    @pl.when(jnp.logical_and(zz == 0, my < 2))
     def _():
         s_far.start()
 
@@ -162,16 +176,16 @@
     def _():
         s_near.start()
 
+    @pl.when(cc == 1)
+    def _():
+        pl.semaphore_wait(barrier, CORES * (len(heads) + 2 - beside - extra))
+        tell(token.at[3], [partner])
+
     @pl.when(cc == 0)
     def _():
-        pl.semaphore_wait(barrier, CORES * (len(heads) + 2 - below - above))
-        tell(token.at[4], [partner])
-
-    @pl.when(cc == 1)
-    def _():
-        pl.semaphore_wait(token.at[4], 1)
-
-    @pl.when(jnp.logical_not(far_soon))
+        pl.semaphore_wait(token.at[3], 1)
+
+    @pl.when(my >= 2)
     def _():
         s_far.start()
 
@@ -195,9 +209,9 @@
     log_st = jnp.log(st)
     tt = jnp.sum(et * td, axis=1, keepdims=True)
 
-    @pl.when(jnp.logical_not(soon))
-    def _():
-        pl.semaphore_wait(token.at[5], below + above)
+    @pl.when(jnp.logical_not(early))
+    def _():
+        pl.semaphore_wait(token.at[4], beside)
 
     pl.semaphore_wait(token.at[0], len(near))
     tell(token.at[1], [plane(0, 2), plane(0, RING_Y - 2)])
@@ -221,9 +235,9 @@
     lower = jnp.broadcast_to(ms + log_ss, (tokens, 128))
     st_all[me] = jnp.concatenate([upper, lower], axis=0).T[:2, :]
     for device in line:
-        remote(st_all.at[me], st_all.at[me], st_sem.at[0], st_sem.at[1], device).start()
+        remote(st_all.at[me], st_all.at[me], ld_sem.at[5], st_sem.at[0], device).start()
     others = st_all.at[pl.ds(0, group - 1)]
-    stats = remote(others, others, st_sem.at[0], st_sem.at[1], partner)
+    stats = remote(others, others, ld_sem.at[5], st_sem.at[0], partner)
 
     stats.wait_recv()
     both = st_all[:, 0, :]
@@ -242,9 +256,9 @@
     pl.semaphore_wait(token.at[2], ring_x - 1)
     away = [(i, j) for i in range(ring_x) for j in range(RING_Y) if (i, j) != (0, 0)]
     for i, j in sorted(away, key=lambda p: -min(p[0], ring_x - p[0]) - min(p[1], RING_Y - p[1])):
-        remote(los_all.at[dp], los_all.at[dp], dp_sem.at[0], dp_sem.at[1], plane(i, j)).start()
+        remote(los_all.at[dp], los_all.at[dp], ld_sem.at[6], dp_sem.at[0], plane(i, j)).start()
     others = los_all.at[pl.ds(0, n_dp - 1)]
-    losses = remote(others, others, dp_sem.at[0], dp_sem.at[1], partner)
+    losses = remote(others, others, ld_sem.at[6], dp_sem.at[0], partner)
     small_ref[0:1, :tokens] = mism
 
     mult = mask * (SOFTENING_HEAT * n_mx * n_my * bc * n_dp * tokens)
@@ -255,8 +269,8 @@
     g_send[...] = (jnp.exp(s_blk - ls) - jnp.exp(t_blk - lt)) * mu
 
     my_far = (1 - lax.div(my, CORES)) * CORES + lax.rem(my, CORES)
-    g_near = remote(g_send, grad_ref.at[my], ag_ssem.at[0], ag_rsem.at[0], {"mx": my, "my": mx})
-    g_far = remote(g_send, grad_ref.at[my], ag_ssem.at[1], ag_rsem.at[1], {"mx": my_far, "my": mx})
+    g_near = remote(g_send, grad_ref.at[my], ld_sem.at[2], ag_rsem.at[0], {"mx": my, "my": mx})
+    g_far = remote(g_send, grad_ref.at[my], ld_sem.at[3], ag_rsem.at[1], {"mx": my_far, "my": mx})
 
     @pl.when(jnp.logical_not(here))
     def _():
@@ -269,7 +283,7 @@
         grad_ref[mx] = g_send[...]
 
     relays = [
-        remote(grad_ref.at[slot], grad_ref.at[slot], rl_sem.at[0], rl_sem.at[1], partner) for slot in (mx, far)
+        remote(grad_ref.at[slot], grad_ref.at[slot], ld_sem.at[4], rl_sem.at[0], partner) for slot in (mx, far)
     ]
 
     @pl.when(jnp.logical_not(here))
@@ -280,7 +294,7 @@
     g_far.wait_recv()
     relays[1].start()
     pair = grad_ref.at[pl.ds(0, 2)]
-    relayed = remote(pair, pair, rl_sem.at[0], rl_sem.at[1], partner)
+    relayed = remote(pair, pair, ld_sem.at[4], rl_sem.at[0], partner)
     relayed.wait_recv()
     losses.wait_recv()
     totals = jnp.sum(los_all[:, 0, :], axis=0, keepdims=True)
@@ -300,17 +314,14 @@
 
 def deliver(small_ref, grad_ref, mism_out, loss_out, grad_out, mism_v, loss_v, sem):
     bc = grad_ref.shape[2]
-    copies = [
-        pltpu.make_async_copy(grad_ref.at[j], grad_out.at[:, j * bc:(j + 1) * bc], sem.at[j])
-        for j in range(grad_ref.shape[0])
-    ]
+    for j in range(grad_ref.shape[0]):
+        pltpu.make_async_copy(grad_ref.at[j], grad_out.at[:, j * bc:(j + 1) * bc], sem.at[0]).start()
+    mism_v[...] = small_ref[0:1, :mism_v.shape[1]]
+    loss_v[...] = small_ref[1:2, 0:1]
+    copies = [pltpu.make_async_copy(mism_v, mism_out, sem.at[1]), pltpu.make_async_copy(loss_v, loss_out, sem.at[2])]
     for c in copies:
         c.start()
-    mism_v[...] = small_ref[0:1, :mism_v.shape[1]]
-    loss_v[...] = small_ref[1:2, 0:1]
-    for src, dst in ((mism_v, mism_out), (loss_v, loss_out)):
-        copies.append(pltpu.make_async_copy(src, dst, sem.at[len(copies)]))
-        copies[-1].start()
+    pltpu.make_async_copy(grad_out, grad_out, sem.at[0]).wait()
     for c in copies:
         c.wait()
 
@@ -335,8 +346,8 @@
             V((2, tokens, bc), f32), V((2, tokens, bc), f32), V((2, tokens, bc), f32),
             V((2, tokens, bc), f32), V((2, tokens, bc), f32), V((tokens, bc), f32),
             V((group, 2, 128), f32), V((n_dp, 1, 128), f32),
-            D((4 + n_mx,)), D((1,)), D((2,)), D((2,)), D((2,)), D((2,)), D((2,)), D((2,)), D((2,)), D((2,)),
-            pltpu.SemaphoreType.REGULAR((7,)),
+            D((4 + n_mx,)), D((1,)), D((2,)), D((2,)), D((2,)), D((1,)), D((1,)), D((1,)),
+            pltpu.SemaphoreType.REGULAR((6,)),
         ],
         compiler_params=pltpu.CompilerParams(
             collective_id=0, has_side_effects=True, vmem_limit_bytes=64_000_000
@@ -351,7 +362,7 @@
         ),
         in_specs=[vm, vm],
         out_specs=(hbm, hbm, hbm),
-        scratch_shapes=[V((1, tokens), f32), V((1, 1), f32), D((2 + n_mx,))],
+        scratch_shapes=[V((1, tokens), f32), V((1, 1), f32), D((3,))],
         compiler_params=pltpu.CompilerParams(vmem_limit_bytes=16 * 1024 * 1024),
     )(*[pltpu.with_memory_space_constraint(x, pltpu.VMEM) for x in held])
     return mism.reshape(tokens), loss.reshape(()), grad

time: 33.4 us -> 33.1 us (level)
  no operation moved by 1% of the time
where the time goes in v10:
time: 33.1 us; the launch traced here: 33 us
  Pallas kernels  32.4 us (98%)
  between operations  0.64 us (2%)
    pallas_call x1, Pallas kernels, shards(): pl.pallas_call(functools.partial(kernel, sizes), out_shape=(V((8, 128), f...  31.6 us
    pallas_call x1, Pallas kernels, shards(): pl.pallas_call(deliver, out_shape=(jax.ShapeDtypeStruct((1, tokens), f32)...  0.73 us

profile of v10, /device:TPU:1, one launch (start us, length us, event | category | flops | bytes accessed | tf_op | source)
XLA Modules:
  0.0 33.0 jit_solution(14863537877250183435)
XLA Ops:
  0.6 31.6 %shard_map.76 = (f32[8,128]{1,0:T(8,128)S(1)}, f32[4,64,256]{2,1,0:T(8,128)S(1)}) custom-call(bf16[64,4608]{1,0:T(8,128)(2,1)} %ts_hbm.1, bf16[4608,256]{1,0:T(8,128)(2,1)} %tw_hbm.1, bf16[64,896]{1,0:T(8,128)(2,1)} %ss_hbm.1, bf16[896,1024]{1,0:T(8,128)(2,1)} %sw_hbm.1, s32[1,64]{1,0:T(1,128)} %bitcast.3), custom_call_target="tpu_custom_call" | custom-call | tf_op jit(solution)/shard_map/pallas_call | solution.py:338
  32.3 0.7 %shard_map.77 = (f32[1,64]{1,0:T(1,128)}, f32[1,1]{1,0:T(1,128)}, f32[64,1024]{1,0:T(8,128)}) custom-call(f32[8,128]{1,0:T(8,128)S(1)} %get-tuple-element.8.small_ref, f32[4,64,256]{2,1,0:T(8,128)S(1)} %get-tuple-element.9.grad_ref), custom_call_target="tpu_custom_call" | custom-call | tf_op jit(solution)/shard_map/pallas_call | solution.py:356

commit v11 on v10

--- a/solution.py
+++ b/solution.py
@@ -19,8 +19,8 @@
     small_ref, grad_ref,
     ts, tw, ss, sw, mask_v,
     d_send, d_recv, own, z_send, z_recv, g_send,
-    st_all, los_all,
-    ld_sem, dd_ssem, dd_rsem, zz_rsem, ag_rsem, rl_sem, st_sem, dp_sem, token,
+    st_all, los_all, cnt_all, g_all,
+    ld_sem, dd_ssem, dd_rsem, zz_rsem, ag_rsem, rl_sem, st_sem, dp_sem, cn_sem, token,
 ):
     n_dp, n_mx, n_my = sizes
     group = n_mx * n_my
@@ -67,16 +67,14 @@
         to = lax.rem(z + k, ring_z)
         return along(k, 1 - (1 - zz) * lax.div(to, n_my) * (1 - lax.div(lax.rem(to, n_my), 2)))
 
-    heads = [head(k) for k in (4, 3, 5, 2, 6)] + [dict(device, mx=zz * CORES + 1) for device in near]
+    upper_high = zz * lax.div(my, 2)
+    low_last = (1 - zz) * lax.div(my, n_my - 1)
+    mute = jnp.logical_and(cc == 0, upper_high == 1)
+    steps = (4, 3, 5, 2, 6)
+    plane_heads = [dict(device, mx=zz * CORES + 1) for device in near]
     beside = below + above
     extra = upper_low * (n_my - 1 + my)
     barrier = pltpu.get_barrier_semaphore()
-    tell(barrier, heads + [along(ring_z - 1, 1 - below), along(1, 1 - above)])
-
-    @pl.when(cc == 1)
-    def _():
-        tell(barrier, [partner])
-
     blocks = [oz * CORES + oc, far, zz * CORES + oc, mx]
     student = [pltpu.make_async_copy(ss_hbm, ss, ld_sem.at[0])]
     for k, block in enumerate(blocks):
@@ -87,7 +85,20 @@
         pltpu.make_async_copy(tw_hbm, tw, ld_sem.at[2 + n_mx]),
     ]
     mask_load = pltpu.make_async_copy(mask_hbm, mask_v, ld_sem.at[3 + n_mx])
-    for c in student:
+    for c in student[:2]:
+        c.start()
+    for k in steps:
+        @pl.when(jnp.logical_not(jnp.logical_and(mute, lax.rem(z + k, ring_z) == n_my - 1)))
+        def _():
+            tell(barrier, [head(k)])
+
+    tell(barrier, plane_heads + [along(ring_z - 1, 1 - below), along(1, 1 - above)])
+
+    @pl.when(cc == 1)
+    def _():
+        tell(barrier, [partner])
+
+    for c in student[2:]:
         c.start()
 
     def dot(k):
@@ -178,7 +189,7 @@
 
     @pl.when(cc == 1)
     def _():
-        pl.semaphore_wait(barrier, CORES * (len(heads) + 2 - beside - extra))
+        pl.semaphore_wait(barrier, CORES * (len(steps) + len(near) + 2 - beside - extra - low_last))
         tell(token.at[3], [partner])
 
     @pl.when(cc == 0)
@@ -198,6 +209,11 @@
         s_near.start()
 
     tell(token.at[0], near)
+
+    @pl.when(mute)
+    def _():
+        for core in range(CORES):
+            tell(token.at[6], [{"mx": core, "my": n_my - 1}])
 
     for c in teacher:
         c.wait()
@@ -215,10 +231,6 @@
 
     pl.semaphore_wait(token.at[0], len(near))
     tell(token.at[1], [plane(0, 2), plane(0, RING_Y - 2)])
-    pl.semaphore_wait(token.at[1], 2)
-    tell(token.at[2], [plane(i, 0) for i in range(1, ring_x)])
-    mask_load.wait()
-    mask = mask_v[...].astype(jnp.float32)
 
     @pl.when(jnp.logical_not(here))
     def _():
@@ -234,11 +246,31 @@
     upper = jnp.where(lane == 0, mt + log_st, kl)
     lower = jnp.broadcast_to(ms + log_ss, (tokens, 128))
     st_all[me] = jnp.concatenate([upper, lower], axis=0).T[:2, :]
+    @pl.when(low_last == 1)
+    def _():
+        pl.semaphore_wait(token.at[6], 2)
+
     for device in line:
         remote(st_all.at[me], st_all.at[me], ld_sem.at[5], st_sem.at[0], device).start()
     others = st_all.at[pl.ds(0, group - 1)]
     stats = remote(others, others, ld_sem.at[5], st_sem.at[0], partner)
 
+    pl.semaphore_wait(token.at[1], 2)
+    tell(token.at[2], [plane(i, 0) for i in range(1, ring_x)])
+    mask_load.wait()
+    mask = mask_v[...].astype(jnp.float32)
+    cnt_all[dp] = jnp.broadcast_to(jnp.sum(mask, axis=1, keepdims=True), cnt_all.shape[1:])
+    pl.semaphore_wait(token.at[2], ring_x - 1)
+    away = [(i, j) for i in range(ring_x) for j in range(RING_Y) if (i, j) != (0, 0)]
+    away.sort(key=lambda p: -min(p[0], ring_x - p[0]) - min(p[1], RING_Y - p[1]))
+
+    def spread(buf, ssem, rsem):
+        for i, j in away:
+            remote(buf.at[dp], buf.at[dp], ssem, rsem, plane(i, j)).start()
+        others = buf.at[pl.ds(0, n_dp - 1)]
+        return remote(others, others, ssem, rsem, partner)
+
+    counts = spread(cnt_all, ld_sem.at[7], cn_sem.at[0])
     stats.wait_recv()
     both = st_all[:, 0, :]
     kls = st_all[:, 1, :][:, :tokens]
@@ -249,16 +281,8 @@
     mism = (SOFTENING_HEAT * SOFTENING_HEAT) * jnp.sum(
         jnp.exp(rel_t) * (kls + (rel_t - rel_s)), axis=0, keepdims=True
     )
-    half = lax.broadcasted_iota(jnp.int32, los_all.shape[1:], 1) < 64
-    los_all[dp] = jnp.where(
-        half, jnp.sum(mask * mism, axis=1, keepdims=True), jnp.sum(mask, axis=1, keepdims=True)
-    )
-    pl.semaphore_wait(token.at[2], ring_x - 1)
-    away = [(i, j) for i in range(ring_x) for j in range(RING_Y) if (i, j) != (0, 0)]
-    for i, j in sorted(away, key=lambda p: -min(p[0], ring_x - p[0]) - min(p[1], RING_Y - p[1])):
-        remote(los_all.at[dp], los_all.at[dp], ld_sem.at[6], dp_sem.at[0], plane(i, j)).start()
-    others = los_all.at[pl.ds(0, n_dp - 1)]
-    losses = remote(others, others, ld_sem.at[6], dp_sem.at[0], partner)
+    los_all[dp] = jnp.broadcast_to(jnp.sum(mask * mism, axis=1, keepdims=True), los_all.shape[1:])
+    losses = spread(los_all, ld_sem.at[6], dp_sem.at[0])
     small_ref[0:1, :tokens] = mism
 
     mult = mask * (SOFTENING_HEAT * n_mx * n_my * bc * n_dp * tokens)
@@ -269,8 +293,8 @@
     g_send[...] = (jnp.exp(s_blk - ls) - jnp.exp(t_blk - lt)) * mu
 
     my_far = (1 - lax.div(my, CORES)) * CORES + lax.rem(my, CORES)
-    g_near = remote(g_send, grad_ref.at[my], ld_sem.at[2], ag_rsem.at[0], {"mx": my, "my": mx})
-    g_far = remote(g_send, grad_ref.at[my], ld_sem.at[3], ag_rsem.at[1], {"mx": my_far, "my": mx})
+    g_near = remote(g_send, g_all.at[my], ld_sem.at[2], ag_rsem.at[0], {"mx": my, "my": mx})
+    g_far = remote(g_send, g_all.at[my], ld_sem.at[3], ag_rsem.at[1], {"mx": my_far, "my": mx})
 
     @pl.when(jnp.logical_not(here))
     def _():
@@ -280,10 +304,10 @@
 
     @pl.when(here)
     def _():
-        grad_ref[mx] = g_send[...]
+        g_all[mx] = g_send[...]
 
     relays = [
-        remote(grad_ref.at[slot], grad_ref.at[slot], ld_sem.at[4], rl_sem.at[0], partner) for slot in (mx, far)
+        remote(g_all.at[slot], g_all.at[slot], ld_sem.at[4], rl_sem.at[0], partner) for slot in (mx, far)
     ]
 
     @pl.when(jnp.logical_not(here))
@@ -293,13 +317,14 @@
     relays[0].start()
     g_far.wait_recv()
     relays[1].start()
-    pair = grad_ref.at[pl.ds(0, 2)]
+    pair = g_all.at[pl.ds(0, 2)]
     relayed = remote(pair, pair, ld_sem.at[4], rl_sem.at[0], partner)
     relayed.wait_recv()
+    counts.wait_recv()
+    count = jnp.sum(cnt_all[:, 0, :], axis=0, keepdims=True)
+    grad_ref[...] = g_all[...] * (1.0 / count[:, 0:1]).reshape(1, 1, 1)
     losses.wait_recv()
-    totals = jnp.sum(los_all[:, 0, :], axis=0, keepdims=True)
-    count = totals[:, 64:65]
-    small_ref[1:2, :] = totals / count
+    small_ref[1:2, :] = jnp.sum(los_all[:, 0, :], axis=0, keepdims=True) / count
 
     @pl.when(jnp.logical_not(here))
     def _():
@@ -307,9 +332,8 @@
         g_near.wait_send()
 
     halves = remote(d_send, d_recv, dd_ssem.at[0], dd_rsem.at[0], partner)
-    for c in [losses, stats, s_far, g_far, halves, relayed]:
+    for c in [counts, losses, stats, s_far, g_far, halves, relayed]:
         c.wait_send()
-    grad_ref[...] = grad_ref[...] * (1.0 / count).reshape(1, 1, 1)
 
 
 def deliver(small_ref, grad_ref, mism_out, loss_out, grad_out, mism_v, loss_v, sem):
@@ -345,9 +369,9 @@
             V((n_mx, sw.shape[0], bc), sw.dtype), V((1, tokens), mask.dtype),
             V((2, tokens, bc), f32), V((2, tokens, bc), f32), V((2, tokens, bc), f32),
             V((2, tokens, bc), f32), V((2, tokens, bc), f32), V((tokens, bc), f32),
-            V((group, 2, 128), f32), V((n_dp, 1, 128), f32),
-            D((4 + n_mx,)), D((1,)), D((2,)), D((2,)), D((2,)), D((1,)), D((1,)), D((1,)),
-            pltpu.SemaphoreType.REGULAR((6,)),
+            V((group, 2, 128), f32), V((n_dp, 1, 128), f32), V((n_dp, 1, 128), f32), V((n_mx, tokens, bc), f32),
+            D((4 + n_mx,)), D((1,)), D((2,)), D((2,)), D((2,)), D((1,)), D((1,)), D((1,)), D((1,)),
+            pltpu.SemaphoreType.REGULAR((7,)),
         ],
         compiler_params=pltpu.CompilerParams(
             collective_id=0, has_side_effects=True, vmem_limit_bytes=64_000_000

time: 33.1 us -> 32.9 us (level)
  no operation moved by 1% of the time
where the time goes in v11:
time: 32.9 us; the launch traced here: 32.8 us
  Pallas kernels  32.1 us (98%)
  between operations  0.64 us (2%)
    pallas_call x1, Pallas kernels, shards(): pl.pallas_call(functools.partial(kernel, sizes), out_shape=(V((8, 128), f...  31.4 us
    pallas_call x1, Pallas kernels, shards(): pl.pallas_call(deliver, out_shape=(jax.ShapeDtypeStruct((1, tokens), f32)...  0.73 us

profile of v11, /device:TPU:1, one launch (start us, length us, event | category | flops | bytes accessed | tf_op | source)
XLA Modules:
  0.0 32.8 jit_solution(10503112274660837574)
XLA Ops:
  0.6 31.4 %shard_map.76 = (f32[8,128]{1,0:T(8,128)S(1)}, f32[4,64,256]{2,1,0:T(8,128)S(1)}) custom-call(bf16[64,4608]{1,0:T(8,128)(2,1)} %ts_hbm.1, bf16[4608,256]{1,0:T(8,128)(2,1)} %tw_hbm.1, bf16[64,896]{1,0:T(8,128)(2,1)} %ss_hbm.1, bf16[896,1024]{1,0:T(8,128)(2,1)} %sw_hbm.1, s32[1,64]{1,0:T(1,128)} %bitcast.3), custom_call_target="tpu_custom_call" | custom-call | tf_op jit(solution)/shard_map/pallas_call | solution.py:362
  32.1 0.7 %shard_map.77 = (f32[1,64]{1,0:T(1,128)}, f32[1,1]{1,0:T(1,128)}, f32[64,1024]{1,0:T(8,128)}) custom-call(f32[8,128]{1,0:T(8,128)S(1)} %get-tuple-element.8.small_ref, f32[4,64,256]{2,1,0:T(8,128)S(1)} %get-tuple-element.9.grad_ref), custom_call_target="tpu_custom_call" | custom-call | tf_op jit(solution)/shard_map/pallas_call | solution.py:380

commit v12 on v11

--- a/solution.py
+++ b/solution.py
@@ -77,9 +77,15 @@
     barrier = pltpu.get_barrier_semaphore()
     blocks = [oz * CORES + oc, far, zz * CORES + oc, mx]
     student = [pltpu.make_async_copy(ss_hbm, ss, ld_sem.at[0])]
+    depth = sw.shape[1]
+    cut = depth // 256 * 128
     for k, block in enumerate(blocks):
         cols = pl.ds(pl.multiple_of(block * bc, bc), bc)
-        student.append(pltpu.make_async_copy(sw_hbm.at[:, cols], sw.at[k], ld_sem.at[1 + k]))
+        rows = pl.ds(0, depth if k else cut)
+        student.append(pltpu.make_async_copy(sw_hbm.at[rows, cols], sw.at[k, rows], ld_sem.at[1 + k]))
+    rest = pl.ds(cut, depth - cut)
+    first_cols = pl.ds(pl.multiple_of(blocks[0] * bc, bc), bc)
+    second_half = pltpu.make_async_copy(sw_hbm.at[rest, first_cols], sw.at[0, rest], ld_sem.at[4 + n_mx])
     teacher = [
         pltpu.make_async_copy(ts_hbm, ts, ld_sem.at[1 + n_mx]),
         pltpu.make_async_copy(tw_hbm, tw, ld_sem.at[2 + n_mx]),
@@ -87,6 +93,7 @@
     mask_load = pltpu.make_async_copy(mask_hbm, mask_v, ld_sem.at[3 + n_mx])
     for c in student[:2]:
         c.start()
+    second_half.start()
     for k in steps:
         @pl.when(jnp.logical_not(jnp.logical_and(mute, lax.rem(z + k, ring_z) == n_my - 1)))
         def _():
@@ -113,7 +120,10 @@
     s_far = remote(z_send.at[1], z_recv.at[1], ld_sem.at[1], zz_rsem.at[1], {"mx": my, "my": far})
 
     student[0].wait()
-    d_send[0] = dot(0)
+    student[1].wait()
+    part = jnp.dot(ss[:, :cut], sw[0, :cut], preferred_element_type=jnp.float32)
+    second_half.wait()
+    d_send[0] = part + jnp.dot(ss[:, cut:], sw[0, cut:], preferred_element_type=jnp.float32)
     for c in teacher:
         c.start()
     mask_load.start()
@@ -370,7 +380,7 @@
             V((2, tokens, bc), f32), V((2, tokens, bc), f32), V((2, tokens, bc), f32),
             V((2, tokens, bc), f32), V((2, tokens, bc), f32), V((tokens, bc), f32),
             V((group, 2, 128), f32), V((n_dp, 1, 128), f32), V((n_dp, 1, 128), f32), V((n_mx, tokens, bc), f32),
-            D((4 + n_mx,)), D((1,)), D((2,)), D((2,)), D((2,)), D((1,)), D((1,)), D((1,)), D((1,)),
+            D((5 + n_mx,)), D((1,)), D((2,)), D((2,)), D((2,)), D((1,)), D((1,)), D((1,)), D((1,)),
             pltpu.SemaphoreType.REGULAR((7,)),
         ],
         compiler_params=pltpu.CompilerParams(

time: 32.9 us -> 32.9 us (level)
  no operation moved by 1% of the time
where the time goes in v12:
time: 32.9 us; the launch traced here: 32.8 us
  Pallas kernels  32.1 us (98%)
  between operations  0.64 us (2%)
    pallas_call x1, Pallas kernels, shards(): pl.pallas_call(functools.partial(kernel, sizes), out_shape=(V((8, 128), f...  31.4 us
    pallas_call x1, Pallas kernels, shards(): pl.pallas_call(deliver, out_shape=(jax.ShapeDtypeStruct((1, tokens), f32)...  0.73 us

profile of v12, /device:TPU:1, one launch (start us, length us, event | category | flops | bytes accessed | tf_op | source)
XLA Modules:
  0.0 32.8 jit_solution(16213964943620136273)
XLA Ops:
  0.6 31.4 %shard_map.76 = (f32[8,128]{1,0:T(8,128)S(1)}, f32[4,64,256]{2,1,0:T(8,128)S(1)}) custom-call(bf16[64,4608]{1,0:T(8,128)(2,1)} %ts_hbm.1, bf16[4608,256]{1,0:T(8,128)(2,1)} %tw_hbm.1, bf16[64,896]{1,0:T(8,128)(2,1)} %ss_hbm.1, bf16[896,1024]{1,0:T(8,128)(2,1)} %sw_hbm.1, s32[1,64]{1,0:T(1,128)} %bitcast.3), custom_call_target="tpu_custom_call" | custom-call | tf_op jit(solution)/shard_map/pallas_call | solution.py:372
  32.1 0.7 %shard_map.77 = (f32[1,64]{1,0:T(1,128)}, f32[1,1]{1,0:T(1,128)}, f32[64,1024]{1,0:T(8,128)}) custom-call(f32[8,128]{1,0:T(8,128)S(1)} %get-tuple-element.8.small_ref, f32[4,64,256]{2,1,0:T(8,128)S(1)} %get-tuple-element.9.grad_ref), custom_call_target="tpu_custom_call" | custom-call | tf_op jit(solution)/shard_map/pallas_call | solution.py:390

commit v13 on v11

--- a/solution.py
+++ b/solution.py
@@ -60,20 +60,23 @@
         to = lax.rem(z + k, ring_z)
         return {"mx": lax.div(to, n_my) * CORES + core, "my": lax.rem(to, n_my)}
 
-    below, above = lax.div(z + ring_z - 1, ring_z), 1 - lax.div(z + 1, ring_z)
+    below = lax.div(z + ring_z - 1, ring_z)
     upper_low = zz * (1 - lax.div(my, 2))
+    low_last = (1 - zz) * lax.div(my, n_my - 1)
 
     def head(k):
         to = lax.rem(z + k, ring_z)
-        return along(k, 1 - (1 - zz) * lax.div(to, n_my) * (1 - lax.div(lax.rem(to, n_my), 2)))
-
+        up = (1 - zz) * lax.div(to, n_my) * (1 - lax.div(lax.rem(to, n_my), 2))
+        return along(k, 1 - up)
+
+    first_chips = (1 - zz) * (1 + below) + n_my * upper_low
+    low_down = below * (1 - lax.div(z, n_my + 1))
+    low_up = 1 - zz
+    rounds = (1 - zz) * (below + 1)
     upper_high = zz * lax.div(my, 2)
-    low_last = (1 - zz) * lax.div(my, n_my - 1)
     mute = jnp.logical_and(cc == 0, upper_high == 1)
     steps = (4, 3, 5, 2, 6)
     plane_heads = [dict(device, mx=zz * CORES + 1) for device in near]
-    beside = below + above
-    extra = upper_low * (n_my - 1 + my)
     barrier = pltpu.get_barrier_semaphore()
     blocks = [oz * CORES + oc, far, zz * CORES + oc, mx]
     student = [pltpu.make_async_copy(ss_hbm, ss, ld_sem.at[0])]
@@ -92,7 +95,7 @@
         def _():
             tell(barrier, [head(k)])
 
-    tell(barrier, plane_heads + [along(ring_z - 1, 1 - below), along(1, 1 - above)])
+    tell(barrier, plane_heads + [along(ring_z - 1, 1 - low_down), along(1, 1 - low_up)])
 
     @pl.when(cc == 1)
     def _():
@@ -120,16 +123,20 @@
 
     @pl.when(cc == 0)
     def _():
-        pl.semaphore_wait(barrier, 1 + CORES * (beside + extra))
+        pl.semaphore_wait(barrier, 1 + CORES * first_chips)
         tell(token.at[3], [partner])
 
-        @pl.when(below == 1)
+        @pl.when(jnp.logical_and(zz == 0, my > 0))
         def _():
             tell(token.at[4], [along(ring_z - 1, core) for core in range(CORES)])
 
-        @pl.when(above == 1)
+        @pl.when(jnp.logical_and(zz == 0, my < n_my - 1))
         def _():
             tell(token.at[4], [along(1, core) for core in range(CORES)])
+
+        @pl.when(z == n_my + 1)
+        def _():
+            tell(token.at[4], [along(ring_z - 2, core) for core in range(CORES)])
 
     @pl.when(cc == 1)
     def _():
@@ -159,37 +166,37 @@
     early = jnp.logical_and(zz == 0, short)
     soon = jnp.logical_or(early, upper_low == 1)
 
+    @pl.when(soon)
+    def _():
+        finish_near()
+
+    @pl.when(early)
+    def _():
+        pl.semaphore_wait(token.at[4], rounds)
+
+    @pl.when(z == 1)
+    def _():
+        tell(token.at[5], [along(ring_z - 1, cc)])
+
+    @pl.when(z == 0)
+    def _():
+        pl.semaphore_wait(token.at[5], 1)
+
+    @pl.when(jnp.logical_and(zz == 0, my < 2))
+    def _():
+        s_far.start()
+
+    @pl.when(jnp.logical_and(soon, jnp.logical_not(here)))
+    def _():
+        s_near.start()
+
     @pl.when(upper_low == 1)
     def _():
         s_far.start()
 
-    @pl.when(soon)
-    def _():
-        finish_near()
-
-    @pl.when(early)
-    def _():
-        pl.semaphore_wait(token.at[4], beside)
-
-    @pl.when(z == 1)
-    def _():
-        tell(token.at[5], [along(ring_z - 1, cc)])
-
-    @pl.when(z == 0)
-    def _():
-        pl.semaphore_wait(token.at[5], 1)
-
-    @pl.when(jnp.logical_and(zz == 0, my < 2))
-    def _():
-        s_far.start()
-
-    @pl.when(jnp.logical_and(soon, jnp.logical_not(here)))
-    def _():
-        s_near.start()
-
     @pl.when(cc == 1)
     def _():
-        pl.semaphore_wait(barrier, CORES * (len(steps) + len(near) + 2 - beside - extra - low_last))
+        pl.semaphore_wait(barrier, CORES * (ring_z - 1 + len(near) - first_chips - low_last))
         tell(token.at[3], [partner])
 
     @pl.when(cc == 0)
@@ -225,9 +232,9 @@
     log_st = jnp.log(st)
     tt = jnp.sum(et * td, axis=1, keepdims=True)
 
-    @pl.when(jnp.logical_not(early))
-    def _():
-        pl.semaphore_wait(token.at[4], beside)
+    @pl.when(jnp.logical_and(zz == 0, jnp.logical_not(early)))
+    def _():
+        pl.semaphore_wait(token.at[4], rounds)
 
     pl.semaphore_wait(token.at[0], len(near))
     tell(token.at[1], [plane(0, 2), plane(0, RING_Y - 2)])

time: 32.9 us -> 33 us (level)
  no operation moved by 1% of the time
where the time goes in v13:
time: 33 us; the launch traced here: 32.8 us
  Pallas kernels  32.2 us (98%)
  between operations  0.64 us (2%)
    pallas_call x1, Pallas kernels, shards(): pl.pallas_call(functools.partial(kernel, sizes), out_shape=(V((8, 128), f...  31.4 us
    pallas_call x1, Pallas kernels, shards(): pl.pallas_call(deliver, out_shape=(jax.ShapeDtypeStruct((1, tokens), f32)...  0.73 us

profile of v13, /device:TPU:1, one launch (start us, length us, event | category | flops | bytes accessed | tf_op | source)
XLA Modules:
  0.0 32.8 jit_solution(10685376450575643379)
XLA Ops:
  0.6 31.4 %shard_map.76 = (f32[8,128]{1,0:T(8,128)S(1)}, f32[4,64,256]{2,1,0:T(8,128)S(1)}) custom-call(bf16[64,4608]{1,0:T(8,128)(2,1)} %ts_hbm.1, bf16[4608,256]{1,0:T(8,128)(2,1)} %tw_hbm.1, bf16[64,896]{1,0:T(8,128)(2,1)} %ss_hbm.1, bf16[896,1024]{1,0:T(8,128)(2,1)} %sw_hbm.1, s32[1,64]{1,0:T(1,128)} %bitcast.3), custom_call_target="tpu_custom_call" | custom-call | tf_op jit(solution)/shard_map/pallas_call | solution.py:369
  32.1 0.7 %shard_map.77 = (f32[1,64]{1,0:T(1,128)}, f32[1,1]{1,0:T(1,128)}, f32[64,1024]{1,0:T(8,128)}) custom-call(f32[8,128]{1,0:T(8,128)S(1)} %get-tuple-element.8.small_ref, f32[4,64,256]{2,1,0:T(8,128)S(1)} %get-tuple-element.9.grad_ref), custom_call_target="tpu_custom_call" | custom-call | tf_op jit(solution)/shard_map/pallas_call | solution.py:387

commit v14 on v11

--- a/solution.py
+++ b/solution.py
@@ -338,8 +338,13 @@
 
 def deliver(small_ref, grad_ref, mism_out, loss_out, grad_out, mism_v, loss_v, sem):
     bc = grad_ref.shape[2]
+    half = grad_ref.shape[1] // 2
     for j in range(grad_ref.shape[0]):
-        pltpu.make_async_copy(grad_ref.at[j], grad_out.at[:, j * bc:(j + 1) * bc], sem.at[0]).start()
+        for r in (0, half):
+            rows = pl.ds(r, half)
+            pltpu.make_async_copy(
+                grad_ref.at[j, rows], grad_out.at[rows, j * bc:(j + 1) * bc], sem.at[0]
+            ).start()
     mism_v[...] = small_ref[0:1, :mism_v.shape[1]]
     loss_v[...] = small_ref[1:2, 0:1]
     copies = [pltpu.make_async_copy(mism_v, mism_out, sem.at[1]), pltpu.make_async_copy(loss_v, loss_out, sem.at[2])]

time: 32.9 us -> 32.9 us (level)
  no operation moved by 1% of the time
where the time goes in v14:
time: 32.9 us; the launch traced here: 32.8 us
  Pallas kernels  32.1 us (98%)
  between operations  0.64 us (2%)
    pallas_call x1, Pallas kernels, shards(): pl.pallas_call(functools.partial(kernel, sizes), out_shape=(V((8, 128), f...  31.4 us
    pallas_call x1, Pallas kernels, shards(): pl.pallas_call(deliver, out_shape=(jax.ShapeDtypeStruct((1, tokens), f32)...  0.72 us

profile of v14, /device:TPU:1, one launch (start us, length us, event | category | flops | bytes accessed | tf_op | source)
XLA Modules:
  0.0 32.8 jit_solution(1281115726920074627)
XLA Ops:
  0.6 31.4 %shard_map.76 = (f32[8,128]{1,0:T(8,128)S(1)}, f32[4,64,256]{2,1,0:T(8,128)S(1)}) custom-call(bf16[64,4608]{1,0:T(8,128)(2,1)} %ts_hbm.1, bf16[4608,256]{1,0:T(8,128)(2,1)} %tw_hbm.1, bf16[64,896]{1,0:T(8,128)(2,1)} %ss_hbm.1, bf16[896,1024]{1,0:T(8,128)(2,1)} %sw_hbm.1, s32[1,64]{1,0:T(1,128)} %bitcast.3), custom_call_target="tpu_custom_call" | custom-call | tf_op jit(solution)/shard_map/pallas_call | solution.py:367
  32.1 0.7 %shard_map.77 = (f32[1,64]{1,0:T(1,128)}, f32[1,1]{1,0:T(1,128)}, f32[64,1024]{1,0:T(8,128)}) custom-call(f32[8,128]{1,0:T(8,128)S(1)} %get-tuple-element.8.small_ref, f32[4,64,256]{2,1,0:T(8,128)S(1)} %get-tuple-element.9.grad_ref), custom_call_target="tpu_custom_call" | custom-call | tf_op jit(solution)/shard_map/pallas_call | solution.py:385
